TPU v7x, 8 devices: a whole 2x2x1 slice. The times are simulated.
8 devices in a mesh: data: 2 (over z, y), seq: 4 (over x, core).
Axes of the slice: x: 2, y: 2, z: 1, core: 2. Of those that a mesh axis runs over, the one named last changes fastest.
Arguments:
- x: bfloat16 [4, 1024, 1024], P('data', 'seq'), parts along dimension 0
- w_in: bfloat16 [1024, 3352], replicated
- dt_bias: float32 [24], replicated
- a_neg: float32 [24], replicated
- d_skip: float32 [24], replicated
- w_out: bfloat16 [1536, 1024], replicated
- w_up1: bfloat16 [1024, 4096], replicated
- w_down1: bfloat16 [2048, 1024], replicated
- w_q: bfloat16 [1024, 8, 64], replicated
- w_kv: bfloat16 [1024, 2, 2, 64], replicated
- w_o: bfloat16 [8, 64, 1024], replicated
- w_up2: bfloat16 [1024, 4096], replicated
- w_down2: bfloat16 [2048, 1024], replicated
Outputs:
- output: bfloat16 [4, 1024, 1024], P('data', 'seq'), parts along dimension 0
There are 2 independent parts. A program takes and returns all parts, laid end to end along the dimension named above; an argument that names none is the same for every part.
All inputs are finite; a program needn't handle non-finite values.
Results may differ from a plain program's by a relative error of at most 0.0141482.
Values are sent between devices in bfloat16 or wider.
A program may use at most 1 GiB of HBM per device.

v0:
```python
import jax
import jax.numpy as jnp
from jax import lax
from jax.sharding import PartitionSpec as P

SSD_BLOCK = 64
NORM_EPS = 1e-6
ROPE_BASE = 10000.0


def rms_norm(values):
    values = values.astype(jnp.float32)
    return values * lax.rsqrt(jnp.mean(values * values, axis=-1, keepdims=True) + NORM_EPS)


def swiglu_mlp(x_loc, w_up, w_down):
    ff_dim = w_down.shape[0]
    normed = rms_norm(x_loc).astype(jnp.bfloat16)
    hidden = jnp.dot(normed, w_up, preferred_element_type=jnp.float32)
    gated_act = (jax.nn.silu(hidden[..., :ff_dim]) * hidden[..., ff_dim:]).astype(jnp.bfloat16)
    return (x_loc.astype(jnp.float32) + jnp.dot(gated_act, w_down, preferred_element_type=jnp.float32)).astype(jnp.bfloat16)


def ssd_local(x_loc, w_in, dt_bias, a_neg, inner):
    n_batch, n_tok = x_loc.shape[0], x_loc.shape[1]
    n_heads = a_neg.shape[0]
    head_p = inner // n_heads
    n_state = (w_in.shape[1] - 2 * inner - n_heads) // 2
    n_blocks = n_tok // SSD_BLOCK
    normed = rms_norm(x_loc).astype(jnp.bfloat16)
    in_proj = jnp.dot(normed, w_in, preferred_element_type=jnp.float32).astype(jnp.bfloat16)
    x_heads = in_proj[..., :inner].reshape(n_batch, n_blocks, SSD_BLOCK, n_heads, head_p)
    gate_z = in_proj[..., inner:2 * inner]
    b_mat = in_proj[..., 2 * inner:2 * inner + n_state].reshape(n_batch, n_blocks, SSD_BLOCK, n_state)
    c_mat = in_proj[..., 2 * inner + n_state:2 * inner + 2 * n_state].reshape(n_batch, n_blocks, SSD_BLOCK, n_state)
    dt_val = jax.nn.softplus(in_proj[..., 2 * inner + 2 * n_state:].astype(jnp.float32) + dt_bias)
    dt_val = dt_val.reshape(n_batch, n_blocks, SSD_BLOCK, n_heads)
    cum_log = jnp.cumsum(dt_val * a_neg, axis=2)
    causal_tri = jnp.arange(SSD_BLOCK)[:, None] >= jnp.arange(SSD_BLOCK)[None, :]
    decay_ts = jnp.exp(jnp.where(causal_tri[:, :, None], cum_log[:, :, :, None, :] - cum_log[:, :, None, :, :], -jnp.inf))
    scores = jnp.einsum('bctn,bcsn->bcts', c_mat, b_mat, preferred_element_type=jnp.float32)
    mix_mat = (scores[..., None] * decay_ts * dt_val[:, :, None, :, :]).astype(jnp.bfloat16)
    y_intra = jnp.einsum('bctsh,bcshp->bcthp', mix_mat, x_heads, preferred_element_type=jnp.float32)
    to_end = jnp.exp(cum_log[:, :, -1:, :] - cum_log) * dt_val
    x_weighted = (x_heads * to_end[..., None]).astype(jnp.bfloat16)
    block_states = jnp.einsum('bcshp,bcsn->bchpn', x_weighted, b_mat, preferred_element_type=jnp.float32)
    block_log = cum_log[:, :, -1, :]
    incl_log = jnp.cumsum(block_log, axis=1)
    excl_log = incl_log - block_log
    lower_mask = jnp.arange(n_blocks)[:, None] > jnp.arange(n_blocks)[None, :]
    trans_mat = jnp.exp(jnp.where(lower_mask[:, :, None], excl_log[:, :, None, :] - incl_log[:, None, :, :], -jnp.inf))
    entry_local = jnp.einsum('bcjh,bjhpn->bchpn', trans_mat, block_states, precision=lax.Precision.HIGHEST)
    end_state = jnp.exp(block_log[:, -1])[..., None, None] * entry_local[:, -1] + block_states[:, -1]
    return (x_heads, gate_z, c_mat, cum_log, y_intra, excl_log, entry_local, end_state, incl_log[:, -1])


def ssd_finish(x_loc, pieces, h_in, d_skip, w_out):
    x_heads, gate_z, c_mat, cum_log, y_intra, excl_log, entry_local = pieces[:7]
    entry_state = entry_local + jnp.exp(excl_log)[..., None, None] * h_in[:, None]
    y_inter = jnp.exp(cum_log)[..., None] * jnp.einsum('bctn,bchpn->bcthp', c_mat, entry_state.astype(jnp.bfloat16), preferred_element_type=jnp.float32)
    y_all = y_intra + y_inter + d_skip[:, None] * x_heads
    y_flat = y_all.reshape(x_loc.shape[0], x_loc.shape[1], w_out.shape[0])
    gated = (rms_norm(y_flat) * jax.nn.silu(gate_z.astype(jnp.float32))).astype(jnp.bfloat16)
    return (x_loc.astype(jnp.float32) + jnp.dot(gated, w_out, preferred_element_type=jnp.float32)).astype(jnp.bfloat16)


def incoming_state(end_state, shard_log, n_dev):
    send_perm = [(idx, idx + 1) for idx in range(n_dev - 1)]
    hop_decay = jnp.exp(shard_log)[..., None, None]

    def hop_step(step_idx, h_in):
        return lax.ppermute(hop_decay * h_in + end_state, 'seq', send_perm)

    return lax.fori_loop(0, n_dev - 1, hop_step, jnp.zeros_like(end_state))


def rope_tables(positions, head_dim):
    half_dim = head_dim // 2
    inv_freq = ROPE_BASE ** (-(jnp.arange(half_dim, dtype=jnp.float32) * 2.0 / head_dim))
    angles = positions.astype(jnp.float32)[:, None] * inv_freq[None, :]
    return jnp.cos(angles), jnp.sin(angles)


def apply_rope(values, cos_t, sin_t):
    half_dim = values.shape[-1] // 2
    first_half = values[..., :half_dim]
    second_half = values[..., half_dim:]
    cos_b = cos_t[:, None, :]
    sin_b = sin_t[:, None, :]
    return jnp.concatenate([first_half * cos_b - second_half * sin_b, second_half * cos_b + first_half * sin_b], axis=-1)


def attention_inputs(x_loc, w_q, w_kv, first_pos):
    n_batch, n_tok = x_loc.shape[0], x_loc.shape[1]
    n_q, head_dim = w_q.shape[1], w_q.shape[2]
    n_kv = w_kv.shape[2]
    normed = rms_norm(x_loc).astype(jnp.bfloat16)
    q_proj = jnp.einsum('bld,dhe->blhe', normed, w_q, preferred_element_type=jnp.float32)
    kv_proj = jnp.einsum('bld,dkhe->kblhe', normed, w_kv, preferred_element_type=jnp.float32)
    cos_t, sin_t = rope_tables(first_pos + jnp.arange(n_tok), head_dim)
    q_rot = apply_rope(q_proj, cos_t, sin_t).astype(jnp.bfloat16)
    q_heads = q_rot.reshape(n_batch, n_tok, n_kv, n_q // n_kv, head_dim)
    kv_pair = jnp.stack([apply_rope(kv_proj[0], cos_t, sin_t), kv_proj[1]]).astype(jnp.bfloat16)
    return q_heads, kv_pair


def init_carry(q_heads):
    stat_shape = (q_heads.shape[0], q_heads.shape[2], q_heads.shape[3], q_heads.shape[1])
    return (jnp.full(stat_shape, -jnp.inf, jnp.float32), jnp.zeros(stat_shape, jnp.float32), jnp.zeros(stat_shape + (q_heads.shape[4],), jnp.float32))


def online_update(acc_state, q_heads, k_blk, v_blk, visible):
    run_max, run_sum, acc_vals = acc_state
    attn_scale = q_heads.shape[-1] ** -0.5
    scores = jnp.einsum('blkgd,bskd->bkgls', q_heads, k_blk, preferred_element_type=jnp.float32) * attn_scale
    if visible is not None:
        scores = jnp.where(visible, scores, -jnp.inf)
    new_max = jnp.maximum(run_max, jnp.max(scores, axis=-1))
    correction = jnp.exp(run_max - new_max)
    prob_vals = jnp.exp(scores - new_max[..., None])
    new_sum = run_sum * correction + jnp.sum(prob_vals, axis=-1)
    new_acc = acc_vals * correction[..., None] + jnp.einsum('bkgls,bskd->bkgld', prob_vals.astype(jnp.bfloat16), v_blk, preferred_element_type=jnp.float32)
    return new_max, new_sum, new_acc


def attention_finish(x_loc, acc_state, w_o):
    attn_vals = (acc_state[2] / acc_state[1][..., None]).astype(jnp.bfloat16)
    w_heads = w_o.reshape(attn_vals.shape[1], attn_vals.shape[2], w_o.shape[1], w_o.shape[2])
    attn_out = jnp.einsum('bkgld,kgde->ble', attn_vals, w_heads, preferred_element_type=jnp.float32)
    return (x_loc.astype(jnp.float32) + attn_out).astype(jnp.bfloat16)


def attention_layer(x_loc, w_q, w_kv, w_o, my_index, n_dev):
    n_tok = x_loc.shape[1]
    q_heads, kv_pair = attention_inputs(x_loc, w_q, w_kv, my_index * n_tok)
    diag_mask = jnp.arange(n_tok)[:, None] >= jnp.arange(n_tok)[None, :]
    acc_state = online_update(init_carry(q_heads), q_heads, kv_pair[0], kv_pair[1], diag_mask)
    send_perm = [(idx, (idx + 1) % n_dev) for idx in range(n_dev)]

    def step_fn(step_idx, loop_state):
        kv_held, acc_inner = loop_state
        kv_held = lax.ppermute(kv_held, 'seq', send_perm)
        acc_inner = lax.cond(step_idx <= my_index, lambda old_state: online_update(old_state, q_heads, kv_held[0], kv_held[1], None), lambda old_state: old_state, acc_inner)
        return kv_held, acc_inner

    final_state = lax.fori_loop(1, n_dev, step_fn, (kv_pair, acc_state))[1]
    return attention_finish(x_loc, final_state, w_o)


def solution(mesh):
    n_dev = mesh.shape['seq']

    def local_fn(x_loc, w_in, dt_bias, a_neg, d_skip, w_out, w_up1, w_down1, w_q, w_kv, w_o, w_up2, w_down2):
        my_index = lax.axis_index('seq')
        pieces = ssd_local(x_loc, w_in, dt_bias, a_neg, w_out.shape[0])
        h_in = incoming_state(pieces[7], pieces[8], n_dev)
        hidden = ssd_finish(x_loc, pieces, h_in, d_skip, w_out)
        hidden = swiglu_mlp(hidden, w_up1, w_down1)
        hidden = attention_layer(hidden, w_q, w_kv, w_o, my_index, n_dev)
        return swiglu_mlp(hidden, w_up2, w_down2)

    seq_spec = P('data', 'seq', None)
    return jax.shard_map(local_fn, mesh=mesh, in_specs=(seq_spec,) + (P(),) * 12, out_specs=seq_spec, check_vma=False)
```

profile of v0, /device:TPU:1, one launch (start us, length us, event | category | flops | bytes accessed | tf_op | source)
XLA Modules:
  0.0 227.7 jit_solution(711455949552816087)
XLA Ops:
  0.0 1.7 fusion.61
  1.7 7.2 %fusion.26 = bf16[2,256,3352]{1,2,0:T(8,128)(2,1)S(1)} fusion(bf16[1024,3352]{0,1:T(8,128)(2,1)} %param.20, bf16[2,256,1024]{2,1,0:T(8,128)(2,1)} %param.19, f32[2,256]{1,0:T(2,128)S(1)} %add_rsqrt_fusion.4), kind=kOutput, calls=%fused_computation.35 | convolution fusion | flops 3518115840 | bytes 11347968 | tf_op jit(solution)/shard_map/dot_general | solution.py:31
  8.9 1.7 copy-done.6
  12.4 1.2 reduce_window_sum.24
  13.6 1.8 exponential_multiply_fusion
  15.4 1.7 copy.50
  17.1 2.7 %slice.90 = bf16[2,256,1536]{1,2,0:T(8,128)(2,1)} slice(bf16[2,256,3352]{1,2,0:T(8,128)(2,1)} %copy-done.6), slice={[0:2], [0:256], [0:1536]} | slice | bytes 3145728 | tf_op jit(solution)/shard_map/slice | solution.py:32
  19.8 5.9 %reshape.192 = bf16[2,4,64,24,64]{2,1,4,3,0:T(4,128)(2,1)} reshape(bf16[2,256,1536]{1,2,0:T(8,128)(2,1)} %slice.90) | data formatting | bytes 3145728 | tf_op jit(solution)/shard_map/reshape | solution.py:32
  25.7 1.7 fusion.134
  27.4 1.0 copy.41
  28.5 5.6 %fusion.43 = f32[2,4,24,64,128]{4,3,2,1,0:T(8,128)} fusion(bf16[2,4,64,128,1]{3,2,4,1,0:T(8,128)(2,1)S(1)} %bitcast.189, f32[2,4,64,24]{2,3,1,0:T(8,128)} %copy.50, bf16[2,4,64,24,64]{2,1,4,3,0:T(4,128)(2,1)} %reshape.192), kind=kOutput, calls=%fused_computation.56 | convolution fusion | flops 203685888 | bytes 8044544 | tf_op jit(solution)/shard_map/bcshp,bcsn->bchpn/dot_general | solution.py:46
  35.5 17.7 %fusion.24 = f32[2,24,64,128,4]{3,4,2,1,0:T(4,128)S(1)} fusion(f32[2,4,24,64,128]{4,3,2,1,0:T(8,128)} %fusion.43, f32[2,4,24]{1,2,0:T(8,128)} %copy.52, f32[2,4,24]{1,2,0:T(8,128)} %copy.51, pred[4,4]{1,0:T(4,128)(4,1)S(1)} %iota_compare_fusion.2), kind=kOutput, calls=%fused_computation.30 | convolution fusion | flops 75499008 | bytes 12584464 | tf_op jit(solution)/shard_map/bcjh,bjhpn->bchpn/dot_general | solution.py:52
  54.0 1.9 copy-done.2
  56.0 2.8 %fusion.80 = f32[2,24,64,128]{3,2,1,0:T(8,128)} fusion(f32[2,4,24,64,128]{4,3,2,1,0:T(8,128)} %fusion.43, f32[2,4,24,64,128]{4,3,2,0,1:T(8,128)S(1)} %bitcast.185, f32[2,24]{1,0:T(2,128)S(1)} %bitcast.209), kind=kLoop, calls=%fused_computation.99 | loop fusion | flops 786432 | bytes 4718784 | tf_op jit(solution)/shard_map/add | solution.py:53
  58.8 1.3 broadcast_in_dim.40
  60.1 75.0 %while.29 = (s32[]{:T(128)}, f32[2,24,64,128]{3,2,1,0:T(8,128)}, f32[2,24,1,1]{1,0,3,2:T(2,128)S(1)}, f32[2,24,64,128]{3,2,1,0:T(8,128)}, s32[]{:T(128)}) while((s32[]{:T(128)}, f32[2,24,64,128]{3,2,1,0:T(8,128)}, f32[2,24,1,1]{1,0,3,2:T(2,128)S(1)}, f32[2,24,64,128]{3,2,1,0:T(8,128)}, s32[]{:T(128)}) %tuple.79), condition=%wide.region_4.5_spmd, body=%wide.region_3.4_spmd.sunk | while | flops 786434 | bytes 11010341 | solution.py:74
  60.1 3.2 %multiply_add_fusion.3 = f32[2,24,64,128]{3,2,1,0:T(8,128)} fusion(f32[2,24,64,128]{3,2,1,0:T(8,128)} %get-tuple-element.342, f32[2,24,64,128]{3,2,1,0:T(8,128)} %get-tuple-element.335, f32[2,24]{1,0:T(2,128)S(1)} %bitcast.206), kind=kLoop, calls=%fused_computation.clone.1 | loop fusion | flops 786432 | bytes 4718784 | tf_op jit(solution)/shard_map/while/body/eval_jaxpr/add | solution.py:72
  63.4 4.5 %collective-permute-start = (f32[2,24,64,128]{3,2,1,0:T(8,128)}, f32[2,24,64,128]{3,2,1,0:T(8,128)}, u32[]{:S(2)}, u32[]{:S(2)}) collective-permute-start(f32[2,24,64,128]{3,2,1,0:T(8,128)} %multiply_add_fusion.3), channel_id=1, source_target_pairs={{0,1},{1,2},{2,3},{4,5},{5,6},{6,7}} | collective-permute-start | bytes 4718600 | tf_op jit(solution)/shard_map/while/body/eval_jaxpr/ppermute | solution.py:72
  67.9 17.3 %collective-permute-done = f32[2,24,64,128]{3,2,1,0:T(8,128)} collective-permute-done((f32[2,24,64,128]{3,2,1,0:T(8,128)}, f32[2,24,64,128]{3,2,1,0:T(8,128)}, u32[]{:S(2)}, u32[]{:S(2)}) %collective-permute-start) | collective-permute-done | bytes 1572896 | tf_op jit(solution)/shard_map/while/body/eval_jaxpr/ppermute | solution.py:72
  85.2 3.2 %multiply_add_fusion.3 = f32[2,24,64,128]{3,2,1,0:T(8,128)} fusion(f32[2,24,64,128]{3,2,1,0:T(8,128)} %get-tuple-element.342, f32[2,24,64,128]{3,2,1,0:T(8,128)} %get-tuple-element.335, f32[2,24]{1,0:T(2,128)S(1)} %bitcast.206), kind=kLoop, calls=%fused_computation.clone.1 | loop fusion | flops 786432 | bytes 4718784 | tf_op jit(solution)/shard_map/while/body/eval_jaxpr/add | solution.py:72
  88.4 4.4 %collective-permute-start = (f32[2,24,64,128]{3,2,1,0:T(8,128)}, f32[2,24,64,128]{3,2,1,0:T(8,128)}, u32[]{:S(2)}, u32[]{:S(2)}) collective-permute-start(f32[2,24,64,128]{3,2,1,0:T(8,128)} %multiply_add_fusion.3), channel_id=1, source_target_pairs={{0,1},{1,2},{2,3},{4,5},{5,6},{6,7}} | collective-permute-start | bytes 4718600 | tf_op jit(solution)/shard_map/while/body/eval_jaxpr/ppermute | solution.py:72
  92.8 17.3 %collective-permute-done = f32[2,24,64,128]{3,2,1,0:T(8,128)} collective-permute-done((f32[2,24,64,128]{3,2,1,0:T(8,128)}, f32[2,24,64,128]{3,2,1,0:T(8,128)}, u32[]{:S(2)}, u32[]{:S(2)}) %collective-permute-start) | collective-permute-done | bytes 1572896 | tf_op jit(solution)/shard_map/while/body/eval_jaxpr/ppermute | solution.py:72
  110.1 3.2 %multiply_add_fusion.3 = f32[2,24,64,128]{3,2,1,0:T(8,128)} fusion(f32[2,24,64,128]{3,2,1,0:T(8,128)} %get-tuple-element.342, f32[2,24,64,128]{3,2,1,0:T(8,128)} %get-tuple-element.335, f32[2,24]{1,0:T(2,128)S(1)} %bitcast.206), kind=kLoop, calls=%fused_computation.clone.1 | loop fusion | flops 786432 | bytes 4718784 | tf_op jit(solution)/shard_map/while/body/eval_jaxpr/add | solution.py:72
  113.4 4.4 %collective-permute-start = (f32[2,24,64,128]{3,2,1,0:T(8,128)}, f32[2,24,64,128]{3,2,1,0:T(8,128)}, u32[]{:S(2)}, u32[]{:S(2)}) collective-permute-start(f32[2,24,64,128]{3,2,1,0:T(8,128)} %multiply_add_fusion.3), channel_id=1, source_target_pairs={{0,1},{1,2},{2,3},{4,5},{5,6},{6,7}} | collective-permute-start | bytes 4718600 | tf_op jit(solution)/shard_map/while/body/eval_jaxpr/ppermute | solution.py:72
  117.8 17.3 %collective-permute-done = f32[2,24,64,128]{3,2,1,0:T(8,128)} collective-permute-done((f32[2,24,64,128]{3,2,1,0:T(8,128)}, f32[2,24,64,128]{3,2,1,0:T(8,128)}, u32[]{:S(2)}, u32[]{:S(2)}) %collective-permute-start) | collective-permute-done | bytes 1572896 | tf_op jit(solution)/shard_map/while/body/eval_jaxpr/ppermute | solution.py:72
  135.1 1.7 copy.40
  136.8 1.8 fusion.136
  140.3 5.8 %fusion.38 = f32[2,4,24,64,64]{4,3,2,1,0:T(8,128)} fusion(f32[2,4,64,24]{2,3,1,0:T(8,128)S(1)} %copy.45, f32[2,4,64,24]{2,3,1,0:T(8,128)} %copy.43, f32[2,4,64,64]{3,2,1,0:T(8,128)} %fusion.136, pred[64,64]{1,0:T(8,128)(4,1)S(1)} %iota_compare_fusion.1, bf16[2,4,64,24,64]{2,1,4,3,0:T(4,128)(2,1)} %reshape.192), kind=kOutput, calls=%fused_computation.51 | convolution fusion | flops 104595456 | bytes 4952064 | tf_op jit(solution)/shard_map/bctsh,bcshp->bcthp/dot_general | solution.py:43
  146.9 7.8 %multiply_reduce_fusion = (f32[2,4,64]{2,1,0:T(4,128)S(1)}, f32[2,4,64,24,64]{2,4,3,1,0:T(8,128)S(1)}) fusion(bf16[2,4,64,24,64]{2,1,4,3,0:T(4,128)(2,1)} %reshape.192, f32[24]{0:T(128)S(1)} %copy-done.8, bf16[2,4,64,128,1]{3,2,4,1,0:T(8,128)(2,1)S(1)} %bitcast.192, f32[2,4,64,24]{2,3,1,0:T(8,128)} %copy.47, f32[2,4,24,64,64]{4,3,2,1,0:T(8,128)} %fusion.38, ...), kind=kOutput, calls=%fused_computation.32 | convolution fusion | flops 211549696 | bytes 15911776 | tf_op jit(solution)/shard_map/bctn,bchpn->bcthp/dot_general | solution.py:60
  154.7 8.4 %copy.57 = f32[2,4,64,24,64]{2,1,4,3,0:T(4,128)} copy(f32[2,4,64,24,64]{2,4,3,1,0:T(8,128)S(1)} %get-tuple-element.238) | data formatting | bytes 6291456 | tf_op jit(solution)/shard_map/add | solution.py:61
  163.1 6.9 %reshape.196 = f32[2,256,1536]{1,2,0:T(8,128)} reshape(f32[2,4,64,24,64]{2,1,4,3,0:T(4,128)} %copy.57) | data formatting | bytes 6291456 | tf_op jit(solution)/shard_map/reshape | solution.py:62
  170.2 4.7 %fusion.64 = (f32[2,256]{1,0:T(2,128)S(1)}, bf16[2,256,1024]{2,1,0:T(8,128)(2,1)S(1)}) fusion(bf16[1536,1024]{1,0:T(8,128)(2,1)S(1)} %copy-done, f32[2,256,1536]{1,2,0:T(8,128)} %reshape.196, bf16[2,256,3352]{1,2,0:T(8,128)(2,1)} %copy-done.6, f32[2,256]{1,0:T(2,128)S(1)} %rsqrt.45, bf16[2,256,1024]{2,1,0:T(8,128)(2,1)} %param.19), kind=kOutput, calls=%fused_computation.86 | convolution fusion | flops 1620049408 | bytes 9965568 | tf_op jit(solution)/shard_map/dot_general | solution.py:64
  174.9 7.7 %fusion.18 = f32[2,256,4096]{2,1,0:T(8,128)S(1)} fusion(bf16[1024,4096]{1,0:T(8,128)(2,1)} %param.25, bf16[2,256,1024]{2,1,0:T(8,128)(2,1)S(1)} %get-tuple-element.240, f32[2,256]{1,0:T(2,128)S(1)} %add_rsqrt_fusion.3), kind=kOutput, calls=%fused_computation.20 | convolution fusion | flops 4296540160 | bytes 17827840 | tf_op jit(solution)/shard_map/dot_general | solution.py:19
  182.6 2.6 %fusion.67 = (f32[2,256]{1,0:T(2,128)S(1)}, bf16[2,256,1024]{2,1,0:T(8,128)(2,1)S(1)}) fusion(bf16[2048,1024]{1,0:T(8,128)(2,1)S(1)} %copy-done.11, f32[2,256,4096]{2,1,0:T(8,128)S(1)} %fusion.18, bf16[2,256,1024]{2,1,0:T(8,128)(2,1)S(1)} %get-tuple-element.240), kind=kOutput, calls=%fused_computation.89 | convolution fusion | flops 2156920320 | bytes 14682112 | tf_op jit(solution)/shard_map/dot_general | solution.py:21
  186.6 1.9 convolution_bitcast_fusion
  190.3 1.1 fusion.96
  191.5 22.7 %while.30 = (s32[]{:T(128)}, bf16[2,2,256,2,64]{2,4,3,1,0:T(8,128)(2,1)S(1)}, f32[2,2,4,256]{3,2,1,0:T(4,128)S(1)}, f32[2,2,4,256]{3,2,1,0:T(4,128)S(1)}, f32[2,...) while((s32[]{:T(128)}, ...), condition=%wide.region_15.16_spmd, body=%wide.region_10.15_spmd.sunk | while | flops 277356544 | bytes 17301740 | solution.py:146
  191.5 2.5 %collective-permute-start.1 = (bf16[2,2,256,2,64]{2,4,3,1,0:T(8,128)(2,1)S(1)}, bf16[2,2,256,2,64]{2,4,3,1,0:T(8,128)(2,1)S(1)}, u32[]{:S(2)}, u32[]{:S(2)}) collective-permute-start(bf16[2,2,256,2,64]{2,4,3,1,0:T(8,128)(2,1)S(1)} %get-tuple-element.353), channel_id=1, source_target_pairs={{0,1},{1,2},{2,3},{3,0},{4,5},{5,6},{6,7},{7,4}} | collective-permute-start | bytes 786440 | tf_op jit(solution)/shard_map/while/body/eval_jaxpr/ppermute | solution.py:142
  194.0 3.3 %collective-permute-done.1 = bf16[2,2,256,2,64]{2,4,3,1,0:T(8,128)(2,1)S(1)} collective-permute-done((bf16[2,2,256,2,64]{2,4,3,1,0:T(8,128)(2,1)S(1)}, bf16[2,2,256,2,64]{2,4,3,1,0:T(8,128)(2,1)S(1)}, u32[]{:S(2)}, u32[]{:S(2)}) %collective-permute-start.1) | collective-permute-done | bytes 262176 | tf_op jit(solution)/shard_map/while/body/eval_jaxpr/ppermute | solution.py:142
  197.3 2.6 %conditional.2 = ((f32[2,2,4,256]{3,2,1,0:T(4,128)S(1)}, f32[2,2,4,256]{3,2,1,0:T(4,128)S(1)}, f32[2,2,4,256,64]{3,4,2,1,0:T(8,128)S(1)})) conditional(s32[]{:T(128)} %convert_element_type.249, (f32[2,2,4,256]{3,2,1,0:T(4,128)S(1)}, f32[2,2,4,256]{3,2,1,0:T(4,128)S(1)}, f32[2,2,4,256,64]{3,4,2,1,0:T(8,128)S(1)}) %tuple.66, ...), branch_computations={%region_11.11_spmd, %region_12.14_spmd} | conditional | flops 277356544 | bytes 15728672 | solution.py:143
  198.9 1.0 fusion.7
  199.9 2.5 %collective-permute-start.1 = (bf16[2,2,256,2,64]{2,4,3,1,0:T(8,128)(2,1)S(1)}, bf16[2,2,256,2,64]{2,4,3,1,0:T(8,128)(2,1)S(1)}, u32[]{:S(2)}, u32[]{:S(2)}) collective-permute-start(bf16[2,2,256,2,64]{2,4,3,1,0:T(8,128)(2,1)S(1)} %get-tuple-element.353), channel_id=1, source_target_pairs={{0,1},{1,2},{2,3},{3,0},{4,5},{5,6},{6,7},{7,4}} | collective-permute-start | bytes 786440 | tf_op jit(solution)/shard_map/while/body/eval_jaxpr/ppermute | solution.py:142
  202.5 3.3 %collective-permute-done.1 = bf16[2,2,256,2,64]{2,4,3,1,0:T(8,128)(2,1)S(1)} collective-permute-done((bf16[2,2,256,2,64]{2,4,3,1,0:T(8,128)(2,1)S(1)}, bf16[2,2,256,2,64]{2,4,3,1,0:T(8,128)(2,1)S(1)}, u32[]{:S(2)}, u32[]{:S(2)}) %collective-permute-start.1) | collective-permute-done | bytes 262176 | tf_op jit(solution)/shard_map/while/body/eval_jaxpr/ppermute | solution.py:142
  205.8 5.1 %collective-permute-start.1 = (bf16[2,2,256,2,64]{2,4,3,1,0:T(8,128)(2,1)S(1)}, bf16[2,2,256,2,64]{2,4,3,1,0:T(8,128)(2,1)S(1)}, u32[]{:S(2)}, u32[]{:S(2)}) collective-permute-start(bf16[2,2,256,2,64]{2,4,3,1,0:T(8,128)(2,1)S(1)} %get-tuple-element.353), channel_id=1, source_target_pairs={{0,1},{1,2},{2,3},{3,0},{4,5},{5,6},{6,7},{7,4}} | collective-permute-start | bytes 786440 | tf_op jit(solution)/shard_map/while/body/eval_jaxpr/ppermute | solution.py:142
  210.9 3.3 %collective-permute-done.1 = bf16[2,2,256,2,64]{2,4,3,1,0:T(8,128)(2,1)S(1)} collective-permute-done((bf16[2,2,256,2,64]{2,4,3,1,0:T(8,128)(2,1)S(1)}, bf16[2,2,256,2,64]{2,4,3,1,0:T(8,128)(2,1)S(1)}, u32[]{:S(2)}, u32[]{:S(2)}) %collective-permute-start.1) | collective-permute-done | bytes 262176 | tf_op jit(solution)/shard_map/while/body/eval_jaxpr/ppermute | solution.py:142
  214.2 2.4 %fusion.70 = (f32[2,256]{1,0:T(2,128)S(1)}, bf16[2,256,1024]{2,1,0:T(8,128)(2,1)S(1)}) fusion(bf16[2,4,64,1024,1]{3,2,1,0,4:T(8,128)(2,1)} %bitcast.210, f32[2,2,4,256,64]{3,4,2,1,0:T(8,128)S(1)} %get-tuple-element.183, f32[2,2,4,256]{3,2,1,0:T(4,128)S(1)} %get-tuple-element.184, bf16[2,256,1024]{2,1,0:T(8,128)(2,1)} %copy-done.14), kind=kOutput, calls=%fused_computation.92 | convolution fusion | flops 540540416 | bytes 4212736 | tf_op jit(solution)/shard_map/bkgld,kgde->ble/dot_general | solution.py:129
  216.6 7.4 %fusion.16 = f32[2,256,4096]{2,1,0:T(8,128)S(1)} fusion(bf16[1024,4096]{1,0:T(8,128)(2,1)} %param.30, bf16[2,256,1024]{2,1,0:T(8,128)(2,1)S(1)} %get-tuple-element.246, f32[2,256]{1,0:T(2,128)S(1)} %add_rsqrt_fusion.1), kind=kOutput, calls=%fused_computation.18 | convolution fusion | flops 4296540160 | bytes 17827840 | tf_op jit(solution)/shard_map/dot_general | solution.py:19
  224.1 3.4 %fusion.72 = bf16[2,256,1024]{2,1,0:T(8,128)(2,1)} fusion(bf16[2,256,1024]{2,1,0:T(8,128)(2,1)S(1)} %get-tuple-element.246, bf16[2048,1024]{1,0:T(8,128)(2,1)S(1)} %copy-done.12, f32[2,256,4096]{2,1,0:T(8,128)S(1)} %fusion.16), kind=kOutput, calls=%fused_computation.94 | convolution fusion | flops 2155347968 | bytes 14680064 | tf_op jit(solution)/shard_map/dot_general | solution.py:21
  (79 shorter events, 11.5 us)
Async XLA Ops:
  0.0 170.2 %copy-start = (bf16[1536,1024]{1,0:T(8,128)(2,1)S(1)}, bf16[1536,1024]{1,0:T(8,128)(2,1)}, u32[]{:S(2)}) copy-start(bf16[1536,1024]{1,0:T(8,128)(2,1)} %param.24) | copy-start | bytes 9437188
  1.7 8.9 %copy-start.9 = (f32[24]{0:T(128)S(1)}, f32[24]{0:T(128)}, u32[]{:S(2)}) copy-start(f32[24]{0:T(128)} %param.21) | copy-start | bytes 292
  1.7 10.0 %copy-start.10 = (f32[24]{0:T(128)S(1)}, f32[24]{0:T(128)}, u32[]{:S(2)}) copy-start(f32[24]{0:T(128)} %param.22) | copy-start | bytes 292
  8.9 1.7 copy-start.6
  10.8 14.9 %copy-start.7 = (f32[2,4,64,24]{2,1,3,0:T(4,128)}, f32[2,4,64,24]{2,1,3,0:T(4,128)S(1)}, u32[]{:S(2)}) copy-start(f32[2,4,64,24]{2,1,3,0:T(4,128)S(1)} %reshape.195) | copy-start | bytes 147460
  11.0 0.7 copy-start.3
  53.2 2.8 %copy-start.2 = (f32[2,24,64,128,4]{3,4,2,1,0:T(4,128)}, f32[2,24,64,128,4]{3,4,2,1,0:T(4,128)S(1)}, u32[]{:S(2)}) copy-start(f32[2,24,64,128,4]{3,4,2,1,0:T(4,128)S(1)} %fusion.24) | copy-start | bytes 18874372
  63.4 21.8 %collective-permute-start = (f32[2,24,64,128]{3,2,1,0:T(8,128)}, f32[2,24,64,128]{3,2,1,0:T(8,128)}, u32[]{:S(2)}, u32[]{:S(2)}) collective-permute-start(f32[2,24,64,128]{3,2,1,0:T(8,128)} %multiply_add_fusion.3), channel_id=1, source_target_pairs={{0,1},{1,2},{2,3},{4,5},{5,6},{6,7}} | collective-permute-start | bytes 4718600 | tf_op jit(solution)/shard_map/while/body/eval_jaxpr/ppermute | solution.py:72
  88.4 21.7 %collective-permute-start = (f32[2,24,64,128]{3,2,1,0:T(8,128)}, f32[2,24,64,128]{3,2,1,0:T(8,128)}, u32[]{:S(2)}, u32[]{:S(2)}) collective-permute-start(f32[2,24,64,128]{3,2,1,0:T(8,128)} %multiply_add_fusion.3), channel_id=1, source_target_pairs={{0,1},{1,2},{2,3},{4,5},{5,6},{6,7}} | collective-permute-start | bytes 4718600 | tf_op jit(solution)/shard_map/while/body/eval_jaxpr/ppermute | solution.py:72
  113.4 21.7 %collective-permute-start = (f32[2,24,64,128]{3,2,1,0:T(8,128)}, f32[2,24,64,128]{3,2,1,0:T(8,128)}, u32[]{:S(2)}, u32[]{:S(2)}) collective-permute-start(f32[2,24,64,128]{3,2,1,0:T(8,128)} %multiply_add_fusion.3), channel_id=1, source_target_pairs={{0,1},{1,2},{2,3},{4,5},{5,6},{6,7}} | collective-permute-start | bytes 4718600 | tf_op jit(solution)/shard_map/while/body/eval_jaxpr/ppermute | solution.py:72
  140.3 5.8 %copy-start.5 = (f32[2,4,64,24]{3,2,1,0:T(8,128)S(1)}, f32[2,4,64,24]{3,2,1,0:T(8,128)}, u32[]{:S(2)}) copy-start(f32[2,4,64,24]{3,2,1,0:T(8,128)} %get-tuple-element.232) | copy-start | bytes 147460
  140.3 6.6 %copy-start.4 = (bf16[2,256,128]{2,1,0:T(8,128)(2,1)S(1)}, bf16[2,256,128]{2,1,0:T(8,128)(2,1)}, u32[]{:S(2)}) copy-start(bf16[2,256,128]{2,1,0:T(8,128)(2,1)} %copy.40) | copy-start | bytes 393220
  140.3 6.6 %copy-start.8 = (f32[24]{0:T(128)S(1)}, f32[24]{0:T(128)}, u32[]{:S(2)}) copy-start(f32[24]{0:T(128)} %param.23) | copy-start | bytes 292
  174.9 7.7 %copy-start.11 = (bf16[2048,1024]{1,0:T(8,128)(2,1)S(1)}, bf16[2048,1024]{1,0:T(8,128)(2,1)}, u32[]{:S(2)}) copy-start(bf16[2048,1024]{1,0:T(8,128)(2,1)} %param.26) | copy-start | bytes 12582916
  182.6 2.7 %copy-start.13 = (bf16[1024,8,64]{0,2,1:T(8,128)(2,1)S(1)}, bf16[1024,8,64]{0,2,1:T(8,128)(2,1)}, u32[]{:S(2)}) copy-start(bf16[1024,8,64]{0,2,1:T(8,128)(2,1)} %param.27) | copy-start | bytes 3145732
  185.2 1.0 copy-start.14
  191.5 5.8 %collective-permute-start.1 = (bf16[2,2,256,2,64]{2,4,3,1,0:T(8,128)(2,1)S(1)}, bf16[2,2,256,2,64]{2,4,3,1,0:T(8,128)(2,1)S(1)}, u32[]{:S(2)}, u32[]{:S(2)}) collective-permute-start(bf16[2,2,256,2,64]{2,4,3,1,0:T(8,128)(2,1)S(1)} %get-tuple-element.353), channel_id=1, source_target_pairs={{0,1},{1,2},{2,3},{3,0},{4,5},{5,6},{6,7},{7,4}} | collective-permute-start | bytes 786440 | tf_op jit(solution)/shard_map/while/body/eval_jaxpr/ppermute | solution.py:142
  199.9 5.8 %collective-permute-start.1 = (bf16[2,2,256,2,64]{2,4,3,1,0:T(8,128)(2,1)S(1)}, bf16[2,2,256,2,64]{2,4,3,1,0:T(8,128)(2,1)S(1)}, u32[]{:S(2)}, u32[]{:S(2)}) collective-permute-start(bf16[2,2,256,2,64]{2,4,3,1,0:T(8,128)(2,1)S(1)} %get-tuple-element.353), channel_id=1, source_target_pairs={{0,1},{1,2},{2,3},{3,0},{4,5},{5,6},{6,7},{7,4}} | collective-permute-start | bytes 786440 | tf_op jit(solution)/shard_map/while/body/eval_jaxpr/ppermute | solution.py:142
  205.8 8.4 %collective-permute-start.1 = (bf16[2,2,256,2,64]{2,4,3,1,0:T(8,128)(2,1)S(1)}, bf16[2,2,256,2,64]{2,4,3,1,0:T(8,128)(2,1)S(1)}, u32[]{:S(2)}, u32[]{:S(2)}) collective-permute-start(bf16[2,2,256,2,64]{2,4,3,1,0:T(8,128)(2,1)S(1)} %get-tuple-element.353), channel_id=1, source_target_pairs={{0,1},{1,2},{2,3},{3,0},{4,5},{5,6},{6,7},{7,4}} | collective-permute-start | bytes 786440 | tf_op jit(solution)/shard_map/while/body/eval_jaxpr/ppermute | solution.py:142
  216.6 7.4 %copy-start.12 = (bf16[2048,1024]{1,0:T(8,128)(2,1)S(1)}, bf16[2048,1024]{1,0:T(8,128)(2,1)}, u32[]{:S(2)}) copy-start(bf16[2048,1024]{1,0:T(8,128)(2,1)} %param.31) | copy-start | bytes 12582916
  224.0 3.4 %copy-start.1 = (bf16[1536,1024]{1,0:T(8,128)(2,1)S(1)}, bf16[1536,1024]{1,0:T(8,128)(2,1)}, u32[]{:S(2)}) copy-start(bf16[1536,1024]{1,0:T(8,128)(2,1)} %param.24) | copy-start | bytes 9437188
where the time goes:
time: 232 us; the launch traced here: 228 us
  matrix products  80.4 us (35%)
  waiting for transfers between devices  61.8 us (27%)
  local copies, waits for them, and re-layouts  41.1 us (18%)
  starting transfers between devices  23.4 us (10%)
  other arithmetic  20.3 us (9%)
    ppermute x3, waiting for transfers between devices, hop_step(): return lax.ppermute(hop_decay * h_in + end_state, 'seq', send_perm)  51.9 us
    dot_general x1, matrix products, ssd_local(): jnp.einsum('bcjh,bjhpn->bchpn', trans_mat, block_states, precision=lax.Pr...  17.7 us
    dot_general x2, matrix products, swiglu_mlp(): hidden = jnp.dot(normed, w_up, preferred_element_type=jnp.float32)  15.1 us
    ppermute x3, starting transfers between devices, hop_step(): return lax.ppermute(hop_decay * h_in + end_state, 'seq', send_perm)  13.3 us
    ppermute x3, starting transfers between devices, step_fn(): kv_held = lax.ppermute(kv_held, 'seq', send_perm)  10.1 us
    ppermute x3, waiting for transfers between devices, step_fn(): kv_held = lax.ppermute(kv_held, 'seq', send_perm)  9.89 us
    add x3, other arithmetic, hop_step(): return lax.ppermute(hop_decay * h_in + end_state, 'seq', send_perm)  9.73 us
    add x1, local copies, waits for them, and re-layouts, ssd_finish(): y_all = y_intra + y_inter + d_skip[:, None] * x_heads  8.43 us
  transfers between devices with their start and end apart: 6, of which 6 were waited for; matrix products, arithmetic and copies ran while one was open for 0% of the time, Pallas kernels for 0%

commit v1 on v0

v1 whole, which is shorter than its diff:
```python
import functools
import jax
import jax.numpy as jnp
import numpy as np
from jax import lax
from jax.experimental import pallas as pl
from jax.experimental.pallas import tpu as pltpu
from jax.sharding import PartitionSpec as P

F32 = jnp.float32
BF16 = jnp.bfloat16
BLK = 64
EPS = 1e-6
ROPE_BASE = 10000.0
NSEQ = 2
TOK = 256
NBLK = TOK // BLK
ROWS = NSEQ * TOK
D = 1024
INNER = 1536
HEADS = 24
NST = 128
FF = 2048
NCH = 3
CHW = INNER // NCH
GW = 256
HD = 64
QH = 8


def dot(a, b):
    return jnp.dot(a, b, preferred_element_type=F32)


def dot_t(a, b):
    return lax.dot_general(a, b, (((1,), (1,)), ((), ())), preferred_element_type=F32)


def hdot(a, b):
    return jnp.dot(a, b, preferred_element_type=F32, precision=lax.Precision.HIGHEST)


def iota(shape, dim):
    return lax.broadcasted_iota(jnp.int32, shape, dim)


def split3(v, lane):
    hi = v.astype(BF16)
    rest = v - hi.astype(F32)
    mid = rest.astype(BF16)
    low = rest - mid.astype(F32)
    return jnp.where(lane < 32, hi.astype(F32), jnp.where(lane < 64, mid.astype(F32), low)).astype(BF16)


def silu(v):
    return v * jax.nn.sigmoid(v)


def kernel(x_h, win_h, bias_r, aneg_r, dskip_r, wout_h, up1_h, down1_h, wq_h, wkv_h, wo_h, up2_h, down2_h, cos_h, sin_h, out_h,
           x_v, u_v, wx_v, wz_v, wt_v, wout_v, up_v, down_v, wq_v, wkv_v, wo_v, cos_v, sin_v,
           xs_v, z_v, b_v, c_v, csp_v, dsp_v, e4_v, bd_v, y_v, ec_v, el_v, dsk_v, bs_v, e_v, hin_v, act_v,
           q_v, kv_v, vt_v, m_v, l_v, acc_v, att_v,
           lsem, osem, st_ssem, st_rsem, k_ssem, k_rsem, v_ssem, v_rsem):
    me = lax.axis_index('seq')
    copies = {}

    def load(name, src, dst, idx):
        copies[name] = pltpu.make_async_copy(src, dst, lsem.at[idx])
        copies[name].start()

    load('x', x_h, x_v, 0)
    load('wx', win_h.at[:, pl.ds(0, INNER)], wx_v, 1)
    load('wt', win_h.at[:, pl.ds(2 * INNER, 2 * NST + HEADS)], wt_v, 2)

    barrier = pltpu.get_barrier_semaphore()
    for off in (1, 2, 3):
        pl.semaphore_signal(barrier, inc=1, device_id={'seq': lax.rem(me + off, 4)}, device_id_type=pl.DeviceIdType.MESH)

    spread = ((iota((HEADS, 128), 1) & 31) == iota((HEADS, 128), 0)) & (iota((HEADS, 128), 1) < 96)
    spread = spread.astype(F32)
    lane8 = iota((8, 128), 1)
    bias3 = hdot(jnp.broadcast_to(bias_r[...], (8, HEADS)), spread)[0:1]
    aneg3 = hdot(jnp.broadcast_to(aneg_r[...], (8, HEADS)), spread)[0:1]
    dsk3 = split3(hdot(jnp.broadcast_to(dskip_r[...], (8, HEADS)), spread), lane8)
    for g in range(INNER // GW):
        cols = pl.ds(g * GW, GW)
        head = (iota((128, GW), 1) + g * GW) >> 6
        row = iota((128, GW), 0)
        e4_v[:, cols] = (((row & 31) == head) & (row < 96)).astype(F32).astype(BF16)
        dsk_v[:, cols] = dot(dsk3, e4_v[:, cols])
    bd_v[...] = ((iota((GW, GW), 0) >> 6) == (iota((GW, GW), 1) >> 6)).astype(F32).astype(BF16)
    for s in range(NSEQ):
        for ch in range(NCH):
            e_v[s, ch] = jnp.zeros((NST, CHW), F32)

    @pl.when(me == 0)
    def _():
        for s in range(NSEQ):
            for ch in range(NCH):
                hin_v[s, ch] = jnp.zeros((NST, CHW), F32)

    def norm_rows(start, count):
        def body(step, carry):
            rows = pl.ds(pl.multiple_of(start + step * 64, 64), 64)
            vals = x_v[rows, :].astype(F32)
            scale = lax.rsqrt(jnp.mean(vals * vals, axis=-1, keepdims=True) + EPS)
            u_v[rows, :] = (vals * scale).astype(BF16)
            return carry
        lax.fori_loop(0, count // 64, body, 0)

    copies['x'].wait()
    norm_rows(0, ROWS)
    load('wz', win_h.at[:, pl.ds(INNER, INNER)], wz_v, 3)
    copies['wx'].wait()
    copies['wt'].wait()
    load('wout', wout_h, wout_v, 4)
    load('up', up1_h, up_v, 5)

    tail = dot(u_v[...], wt_v[...])
    b_v[...] = tail[:, :NST].astype(BF16)
    c_v[...] = tail[:, NST:2 * NST].astype(BF16)
    r_bf = tail[:, 2 * NST:].astype(BF16)
    spread_bf = spread.astype(BF16)
    tri = (iota((TOK, TOK), 0) >= iota((TOK, TOK), 1)) & ((iota((TOK, TOK), 0) >> 6) == (iota((TOK, TOK), 1) >> 6))
    tri = tri.astype(F32)
    lane = iota((TOK, 128), 1)
    for s in range(NSEQ):
        pre = dot(r_bf[s * TOK:(s + 1) * TOK], spread_bf) + bias3
        dt = jnp.maximum(pre, 0.0) + jnp.log1p(jnp.exp(-jnp.abs(pre)))
        cum = hdot(tri, dt * aneg3)
        csp_v[s * TOK:(s + 1) * TOK, :] = split3(cum, lane)
        dsp_v[s * TOK:(s + 1) * TOK, :] = split3(dt, lane)

    def proj_x(j, carry):
        cols = pl.ds(pl.multiple_of(j * 512, 512), 512)
        xs_v[:, cols] = dot(u_v[...], wx_v[:, cols]).astype(BF16)
        return carry
    lax.fori_loop(0, INNER // 512, proj_x, 0)

    t_idx = iota((BLK, GW), 0)
    s_idx = iota((BLK, GW), 1) & (BLK - 1)

    def block_step(s):
        def body(b, carry):
            i = s * NBLK + b
            rows = pl.ds(pl.multiple_of(i * BLK, BLK), BLK)
            cs = csp_v[rows, :]
            ds = dsp_v[rows, :]
            bb = b_v[rows, :]
            cb = c_v[rows, :]
            b4 = jnp.concatenate([bb] * 4, axis=0)
            sc4 = dot_t(cb, b4)
            bt = bb.astype(F32).T.astype(BF16)
            for g in range(INNER // GW):
                ch, off = g // 2, (g % 2) * GW
                cols = pl.ds(g * GW, GW)
                ce = dot(cs, e4_v[:, cols])
                de = dot(ds, e4_v[:, cols])
                crow = jnp.sum(jnp.where(t_idx == s_idx, ce, 0.0), axis=0, keepdims=True)
                drow = jnp.sum(jnp.where(t_idx == s_idx, de, 0.0), axis=0, keepdims=True)
                decay = jnp.exp(jnp.where(t_idx >= s_idx, ce - crow, -jnp.inf))
                mix = (sc4 * decay * drow).astype(BF16)
                xg = xs_v[rows, cols]
                xw = xg.astype(F32)
                xbd = jnp.concatenate([xg] * 4, axis=0) * bd_v[...]
                y_v[rows, cols] = dot(mix, xbd) + dsk_v[0:1, cols] * xw
                last = ce[BLK - 1:BLK, :]
                to_end = jnp.exp(last - ce) * de
                state = dot(bt, (xw * to_end).astype(BF16))
                el = jnp.exp(last)
                bs_v[i, ch, :, off:off + GW] = state
                ec_v[rows, cols] = jnp.exp(ce)
                el_v[pl.ds(pl.multiple_of(i * 8, 8), 8), cols] = jnp.broadcast_to(el, (8, GW))
                e_v[s, ch, :, off:off + GW] = el * e_v[s, ch, :, off:off + GW] + state
            return carry
        return body

    def st_copy(s, ch, dst):
        src = e_v.at[s, ch]
        return pltpu.make_async_remote_copy(src_ref=src, dst_ref=hin_v.at[s, ch], send_sem=st_ssem.at[s, ch], recv_sem=st_rsem.at[s, ch],
                                            device_id={'seq': dst}, device_id_type=pl.DeviceIdType.MESH)

    def chain(s, ch, dst):
        cols = pl.ds(ch * CHW, CHW)
        total = el_v[(s * NBLK) * 8:(s * NBLK) * 8 + 1, cols]
        for b in range(1, NBLK):
            total = total * el_v[(s * NBLK + b) * 8:(s * NBLK + b) * 8 + 1, cols]
        e_v[s, ch] = total * hin_v[s, ch] + e_v[s, ch]
        st_copy(s, ch, dst).start()

    def first_send(s):
        @pl.when(me == 0)
        def _():
            for ch in range(NCH):
                st_copy(s, ch, 1).start()

    def relay(s):
        @pl.when(me == 1)
        def _():
            for ch in range(NCH):
                st_copy(s, ch, 2).wait_recv()
                chain(s, ch, 2)

    lax.fori_loop(0, NBLK, block_step(0), 0)
    pl.semaphore_wait(barrier, 3)
    first_send(0)
    lax.fori_loop(0, NBLK // 2, block_step(1), 0)
    relay(0)
    lax.fori_loop(NBLK // 2, NBLK, block_step(1), 0)
    first_send(1)
    load('down', down1_h, down_v, 6)
    load('wq', wq_h, wq_v, 7)
    load('wkv', wkv_h, wkv_v, 8)
    load('wo', wo_h, wo_v, 9)
    tab = pl.ds(pl.multiple_of(me * TOK, TOK), TOK)
    load('cos', cos_h.at[tab, :], cos_v, 10)
    load('sin', sin_h.at[tab, :], sin_v, 11)
    copies['wz'].wait()

    def proj_z(j, carry):
        cols = pl.ds(pl.multiple_of(j * 512, 512), 512)
        z_v[:, cols] = dot(u_v[...], wz_v[:, cols]).astype(BF16)
        return carry
    lax.fori_loop(0, INNER // 512, proj_z, 0)
    relay(1)

    def ssd_finish(s):
        @pl.when(me == 1)
        def _():
            pass

        @pl.when(me == 2)
        def _():
            for ch in range(NCH):
                st_copy(s, ch, 3).wait_recv()
                chain(s, ch, 3)

        @pl.when(me == 3)
        def _():
            for ch in range(NCH):
                st_copy(s, ch, 3).wait_recv()

        def body(b, carry):
            i = s * NBLK + b
            rows = pl.ds(pl.multiple_of(i * BLK, BLK), BLK)
            cb = c_v[rows, :]
            for ch in range(NCH):
                cols = pl.ds(ch * CHW, CHW)
                held = hin_v[s, ch]
                y_v[rows, cols] = y_v[rows, cols] + ec_v[rows, cols] * dot(cb, held.astype(BF16))
                el = el_v[pl.ds(pl.multiple_of(i * 8, 8), 8), cols][0:1]
                hin_v[s, ch] = el * held + bs_v[i, ch]
            ssq = jnp.zeros((BLK, 1), F32)
            for ch in range(NCH):
                yv = y_v[rows, ch * CHW:(ch + 1) * CHW]
                ssq = ssq + jnp.sum(yv * yv, axis=-1, keepdims=True)
            scale = lax.rsqrt(ssq * (1.0 / INNER) + EPS)
            for ch in range(NCH):
                cols = pl.ds(ch * CHW, CHW)
                xs_v[rows, cols] = (y_v[rows, cols] * scale * silu(z_v[rows, cols].astype(F32))).astype(BF16)
            return carry
        lax.fori_loop(0, NBLK, body, 0)

        rows = pl.ds(s * TOK, TOK)

        def out_proj(j, carry):
            cols = pl.ds(pl.multiple_of(j * 512, 512), 512)
            x_v[rows, cols] = (x_v[rows, cols].astype(F32) + dot(xs_v[rows, :], wout_v[:, cols])).astype(BF16)
            return carry
        lax.fori_loop(0, D // 512, out_proj, 0)

    def mlp_up(start, count, width):
        rows = pl.ds(start, count)

        def body(j, carry):
            c0 = pl.multiple_of(j * width, width)
            gate = dot(u_v[rows, :], up_v[:, pl.ds(c0, width)])
            up = dot(u_v[rows, :], up_v[:, pl.ds(FF + c0, width)])
            act_v[rows, pl.ds(c0, width)] = (silu(gate) * up).astype(BF16)
            return carry
        lax.fori_loop(0, FF // width, body, 0)

    def mlp_down(start, count, width):
        rows = pl.ds(start, count)

        def body(j, carry):
            cols = pl.ds(pl.multiple_of(j * width, width), width)
            x_v[rows, cols] = (x_v[rows, cols].astype(F32) + dot(act_v[rows, :], down_v[:, cols])).astype(BF16)
            return carry
        lax.fori_loop(0, D // width, body, 0)

    def rope(vals):
        low = (iota(vals.shape, 1) & 63) < 32
        swapped = jnp.where(low, pltpu.roll(vals, 96, 1), pltpu.roll(vals, 32, 1))
        return vals * cos_v[...] + swapped * sin_v[...]

    def k_copy(s, piece, slot, dst):
        return pltpu.make_async_remote_copy(src_ref=kv_v.at[s, piece], dst_ref=kv_v.at[s, piece], send_sem=k_ssem.at[s, slot], recv_sem=k_rsem.at[s, piece],
                                            device_id={'seq': dst}, device_id_type=pl.DeviceIdType.MESH)

    def v_copy(s, piece, slot, dst):
        return pltpu.make_async_remote_copy(src_ref=vt_v.at[s, piece], dst_ref=vt_v.at[s, piece], send_sem=v_ssem.at[s, slot], recv_sem=v_rsem.at[s, piece],
                                            device_id={'seq': dst}, device_id_type=pl.DeviceIdType.MESH)

    def kv_send(s, piece, slot, dst):
        k_copy(s, piece, slot, dst).start()
        v_copy(s, piece, slot, dst).start()

    def kv_wait(s, piece):
        k_copy(s, piece, 0, 0).wait_recv()
        v_copy(s, piece, 0, 0).wait_recv()

    def kv_sent(s, piece, slot, dst):
        k_copy(s, piece, slot, dst).wait_send()
        v_copy(s, piece, slot, dst).wait_send()

    def qkv(s):
        rows = pl.ds(s * TOK, TOK)
        norm_rows(s * TOK, TOK)
        kv = dot(u_v[rows, :], wkv_v[...])
        kv_v[s, me] = rope(kv[:, :128]).astype(BF16)
        vt_v[s, me] = kv[:, 128:].T.astype(BF16)
        q = dot(u_v[rows, :], wq_v[...])
        for pair in range(QH // 2):
            rot = rope(q[:, pair * 128:(pair + 1) * 128]).astype(BF16)
            q_v[2 * pair] = rot[:, :HD]
            q_v[2 * pair + 1] = rot[:, HD:]

        @pl.when(me == 0)
        def _():
            kv_send(s, 0, 0, 1)
            kv_send(s, 0, 1, 2)

        @pl.when(me == 1)
        def _():
            kv_send(s, 1, 0, 3)

        @pl.when(me == 2)
        def _():
            kv_send(s, 2, 0, 3)
            kv_wait(s, 0)
            kv_send(s, 0, 1, 3)

        @pl.when(me == 3)
        def _():
            kv_wait(s, 1)
            kv_send(s, 1, 0, 2)

    def attend(s, piece, first):
        causal = iota((TOK, TOK), 0) <= iota((TOK, TOK), 1)
        keys = kv_v[s, piece]
        vals = vt_v[s, piece]
        for h in range(QH):
            g = h // 4
            k_g = keys[:, g * HD:(g + 1) * HD]
            v_g = vals[g * HD:(g + 1) * HD, :]
            sc = dot_t(k_g, q_v[h]) * 0.125
            if first:
                sc = jnp.where(causal, sc, -jnp.inf)
                top = jnp.max(sc, axis=0, keepdims=True)
                prob = jnp.exp(sc - top)
                l_v[h:h + 1, :] = jnp.sum(prob, axis=0, keepdims=True)
                acc_v[h] = dot(v_g, prob.astype(BF16))
            else:
                old = m_v[h:h + 1, :]
                top = jnp.maximum(old, jnp.max(sc, axis=0, keepdims=True))
                fix = jnp.exp(old - top)
                prob = jnp.exp(sc - top)
                l_v[h:h + 1, :] = l_v[h:h + 1, :] * fix + jnp.sum(prob, axis=0, keepdims=True)
                acc_v[h] = acc_v[h] * fix + dot(v_g, prob.astype(BF16))
            m_v[h:h + 1, :] = top

    def attention(s):
        attend(s, me, True)
        for piece in range(3):
            @pl.when(me > piece)
            def _(piece=piece):
                if piece == 0:
                    @pl.when(me != 2)
                    def _():
                        kv_wait(s, 0)
                elif piece == 1:
                    @pl.when(me == 2)
                    def _():
                        kv_wait(s, 1)
                else:
                    kv_wait(s, 2)
                attend(s, piece, False)
        rows = pl.ds(s * TOK, TOK)
        for pair in range(QH // 2):
            top = acc_v[2 * pair] / l_v[2 * pair:2 * pair + 1, :]
            bot = acc_v[2 * pair + 1] / l_v[2 * pair + 1:2 * pair + 2, :]
            att_v[:, pair * 128:(pair + 1) * 128] = jnp.concatenate([top, bot], axis=0).T.astype(BF16)

        def o_proj(j, carry):
            cols = pl.ds(pl.multiple_of(j * 512, 512), 512)
            x_v[rows, cols] = (x_v[rows, cols].astype(F32) + dot(att_v[...], wo_v[:, cols])).astype(BF16)
            return carry
        lax.fori_loop(0, D // 512, o_proj, 0)

    copies['wout'].wait()
    ssd_finish(0)
    norm_rows(0, TOK)
    copies['up'].wait()
    mlp_up(0, TOK, 512)
    copies['down'].wait()
    mlp_down(0, TOK, 512)
    for name in ('wq', 'wkv', 'wo', 'cos', 'sin'):
        copies[name].wait()
    qkv(0)
    attention(0)
    ssd_finish(1)
    norm_rows(TOK, TOK)
    mlp_up(TOK, TOK, 512)
    load('up', up2_h, up_v, 5)
    mlp_down(TOK, TOK, 512)
    load('down', down2_h, down_v, 6)
    qkv(1)
    attention(1)
    norm_rows(0, ROWS)
    copies['up'].wait()
    mlp_up(0, ROWS, 256)
    copies['down'].wait()
    mlp_down(0, ROWS, 256)
    done = pltpu.make_async_copy(x_v, out_h, osem)
    done.start()

    @pl.when(me < 3)
    def _():
        for s in range(NSEQ):
            for ch in range(NCH):
                st_copy(s, ch, 0).wait_send()
    for s in range(NSEQ):
        kv_sent(s, 0, 0, 0)

        @pl.when((me == 0) | (me == 2))
        def _():
            kv_sent(s, 0, 1, 0)
    done.wait()


def rope_tables(seq_len):
    inv = (np.float32(ROPE_BASE) ** (-(np.arange(32, dtype=np.float32) * np.float32(2.0) / np.float32(HD)))).astype(np.float32)
    ang = (np.arange(seq_len, dtype=np.float32)[:, None] * inv[None, :]).astype(np.float32).astype(np.float64)
    cos = np.cos(ang).astype(np.float32)
    sin = np.sin(ang).astype(np.float32)
    return np.tile(cos, (1, 4)), np.concatenate([-sin, sin, -sin, sin], axis=1)


def solution(mesh):
    n_dev = mesh.shape['seq']
    cos_t, sin_t = rope_tables(n_dev * TOK)
    any_spec = pl.BlockSpec(memory_space=pl.ANY)
    vm_spec = pl.BlockSpec(memory_space=pltpu.VMEM)
    vm = pltpu.VMEM
    call = pl.pallas_call(
        kernel,
        out_shape=jax.ShapeDtypeStruct((ROWS, D), BF16),
        in_specs=[any_spec, any_spec, vm_spec, vm_spec, vm_spec] + [any_spec] * 10,
        out_specs=any_spec,
        scratch_shapes=[
            vm((ROWS, D), BF16), vm((ROWS, D), BF16), vm((D, INNER), BF16), vm((D, INNER), BF16), vm((D, 2 * NST + HEADS), BF16),
            vm((INNER, D), BF16), vm((D, 2 * FF), BF16), vm((FF, D), BF16), vm((D, QH * HD), BF16), vm((D, 256), BF16), vm((QH * HD, D), BF16),
            vm((TOK, 128), F32), vm((TOK, 128), F32),
            vm((ROWS, INNER), BF16), vm((ROWS, INNER), BF16), vm((ROWS, NST), BF16), vm((ROWS, NST), BF16),
            vm((ROWS, 128), BF16), vm((ROWS, 128), BF16), vm((128, INNER), BF16), vm((GW, GW), BF16),
            vm((ROWS, INNER), F32), vm((ROWS, INNER), F32), vm((NSEQ * NBLK * 8, INNER), F32), vm((8, INNER), F32),
            vm((NSEQ * NBLK, NCH, NST, CHW), F32), vm((NSEQ, NCH, NST, CHW), F32), vm((NSEQ, NCH, NST, CHW), F32), vm((ROWS, FF), BF16),
            vm((QH, TOK, HD), BF16), vm((NSEQ, 4, TOK, 128), BF16), vm((NSEQ, 4, 128, TOK), BF16),
            vm((QH, TOK), F32), vm((QH, TOK), F32), vm((QH, HD, TOK), F32), vm((TOK, QH * HD), BF16),
            pltpu.SemaphoreType.DMA((12,)), pltpu.SemaphoreType.DMA, pltpu.SemaphoreType.DMA((NSEQ, NCH)), pltpu.SemaphoreType.DMA((NSEQ, NCH)),
            pltpu.SemaphoreType.DMA((NSEQ, 2)), pltpu.SemaphoreType.DMA((NSEQ, 4)), pltpu.SemaphoreType.DMA((NSEQ, 2)), pltpu.SemaphoreType.DMA((NSEQ, 4)),
        ],
        compiler_params=pltpu.CompilerParams(collective_id=0, has_side_effects=True, vmem_limit_bytes=67_000_000),
        name='layer_stack',
    )

    def local_fn(x_loc, w_in, dt_bias, a_neg, d_skip, w_out, w_up1, w_down1, w_q, w_kv, w_o, w_up2, w_down2):
        out = call(x_loc.reshape(ROWS, D), w_in, dt_bias.reshape(1, HEADS), a_neg.reshape(1, HEADS), d_skip.reshape(1, HEADS), w_out, w_up1, w_down1,
                   w_q.reshape(D, QH * HD), w_kv.reshape(D, 256), w_o.reshape(QH * HD, D), w_up2, w_down2, jnp.asarray(cos_t), jnp.asarray(sin_t))
        return out.reshape(x_loc.shape)

    seq_spec = P('data', 'seq', None)
    return jax.shard_map(local_fn, mesh=mesh, in_specs=(seq_spec,) + (P(),) * 12, out_specs=seq_spec, check_vma=False)
```

time: 232 us -> 92.8 us (0.40)
  the two profiles are of different devices: /device:TPU:1 before, /device:TPU:7 now
where the time goes in v1:
time: 92.8 us; the launch traced here: 92.4 us
  Pallas kernels  76 us (82%)
  local copies, waits for them, and re-layouts  16.3 us (18%)
    pallas_call x1, Pallas kernels, local_fn(): call(x_loc.reshape(ROWS, D), w_in, dt_bias.reshape(1, HEADS), a_neg.resha...  76 us
    unnamed x2, local copies, waits for them, and re-layouts  11.9 us
    reshape x1, local copies, waits for them, and re-layouts, local_fn(): w_q.reshape(D, QH * HD)  2.27 us
    reshape x1, local copies, waits for them, and re-layouts, local_fn(): w_kv.reshape(D, 256)  2.09 us

profile of v1, /device:TPU:7, one launch (start us, length us, event | category | flops | bytes accessed | tf_op | source)
XLA Modules:
  0.0 92.4 jit_solution(10344288993950725316)
XLA Ops:
  0.0 2.1 %copy.21.wkv_h = bf16[1024,256]{1,0:T(8,128)(2,1)} copy(bf16[1024,256]{0,1:T(8,128)(2,1)} %bitcast.12) | data formatting | bytes 1048576 | tf_op jit(solution)/shard_map/reshape | solution.py:480
  2.1 2.3 %copy.20.wq_h = bf16[1024,512]{1,0:T(8,128)(2,1)} copy(bf16[1024,512]{0,1:T(8,128)(2,1)} %bitcast.11) | data formatting | bytes 2097152 | tf_op jit(solution)/shard_map/reshape | solution.py:480
  4.4 9.7 %copy.19.win_h = bf16[1024,3352]{1,0:T(8,128)(2,1)} copy(bf16[1024,3352]{0,1:T(8,128)(2,1)} %param.16) | data formatting | bytes 13729792 | tf_op args[1]
  14.0 76.0 %layer_stack.1 = bf16[512,1024]{1,0:T(8,128)(2,1)} custom-call(bf16[512,1024]{1,0:T(8,128)(2,1)} %bitcast.9, bf16[1024,3352]{1,0:T(8,128)(2,1)} %copy.19.win_h, f32[1,24]{1,0:T(1,128)} %bitcast.13, f32[1,24]{1,0:T(1,128)} %bitcast.14, f32[1,24]{1,0:T(1,128)} %bitcast.15, bf16[1536,1024]{1,0:T(8,128)(2,1)} %wout_h.1, bf16[1024,4096]{1,0:T(8,128)(2,1)} %up1_h.1, ...), custom_call_target="tpu_custom_call" | custom-call | tf_op jit(solution)/shard_map/layer_stack/pallas_call | solution.py:479
  90.1 2.3 %copy.23 = bf16[2,256,1024]{2,1,0:T(8,128)(2,1)} copy(bf16[2,256,1024]{2,1,0:T(8,128)(2,1)} %bitcast.8) | data formatting | bytes 2097152

commit v2 on v1

v2 whole, which is shorter than its diff:
```python
import functools
import jax
import jax.numpy as jnp
import numpy as np
from jax import lax
from jax.experimental import pallas as pl
from jax.experimental.pallas import tpu as pltpu
from jax.sharding import PartitionSpec as P

F32 = jnp.float32
BF16 = jnp.bfloat16
BLK = 64
EPS = 1e-6
ROPE_BASE = 10000.0
NSEQ = 2
TOK = 256
NBLK = TOK // BLK
ROWS = NSEQ * TOK
D = 1024
INNER = 1536
HEADS = 24
NST = 128
FF = 2048
NCH = 3
CHW = INNER // NCH
GW = 256
HD = 64
QH = 8


def dot(a, b):
    return jnp.dot(a, b, preferred_element_type=F32)


def dot_t(a, b):
    return lax.dot_general(a, b, (((1,), (1,)), ((), ())), preferred_element_type=F32)


def hdot(a, b):
    return jnp.dot(a, b, preferred_element_type=F32, precision=lax.Precision.HIGHEST)


def iota(shape, dim):
    return lax.broadcasted_iota(jnp.int32, shape, dim)


def split3(v, lane):
    hi = v.astype(BF16)
    rest = v - hi.astype(F32)
    mid = rest.astype(BF16)
    low = rest - mid.astype(F32)
    return jnp.where(lane < 32, hi.astype(F32), jnp.where(lane < 64, mid.astype(F32), low)).astype(BF16)


def silu(v):
    return v * jax.nn.sigmoid(v)


def kernel(x_h, win_h, bias_r, aneg_r, dskip_r, wout_h, up1_h, down1_h, wq_h, wkv_h, wo_h, up2_h, down2_h, cos_h, sin_h, out_h,
           x_v, u_v, wx_v, wz_v, wt_v, wout_v, up_v, down_v, wqkv_v, wo_v, cos_v, sin_v,
           xs_v, z_v, b_v, c_v, csp_v, dsp_v, e4_v, bd_v, y_v, ec_v, de_v, el_v, dsk_v, bs_v, e_v, hin_v, act_v,
           qz_v, kv_v, vt_v, m_v, l_v, acc_v, att_v, sc_v, pr_v,
           lsem, osem, st_ssem, st_rsem, k_ssem, k_rsem, v_ssem, v_rsem):
    me = lax.axis_index('seq')
    copies = {}

    def load(name, src, dst, idx):
        copies[name] = pltpu.make_async_copy(src, dst, lsem.at[idx])
        copies[name].start()

    load('x', x_h, x_v, 0)
    load('wt', win_h.at[pl.ds(2 * INNER, 2 * NST + HEADS), :], wt_v, 1)
    for ch in range(NCH):
        load('wx%d' % ch, win_h.at[pl.ds(ch * CHW, CHW), :], wx_v.at[pl.ds(ch * CHW, CHW), :], 2 + ch)
    load('wz', win_h.at[pl.ds(INNER, INNER), :], wz_v, 5)

    barrier = pltpu.get_barrier_semaphore()
    for off in (1, 2, 3):
        pl.semaphore_signal(barrier, inc=1, device_id={'seq': lax.rem(me + off, 4)}, device_id_type=pl.DeviceIdType.MESH)

    spread = ((iota((HEADS, 128), 1) & 31) == iota((HEADS, 128), 0)) & (iota((HEADS, 128), 1) < 96)
    spread = spread.astype(F32)
    lane8 = iota((8, 128), 1)
    bias3 = hdot(jnp.broadcast_to(bias_r[...], (8, HEADS)), spread)[0:1]
    aneg3 = hdot(jnp.broadcast_to(aneg_r[...], (8, HEADS)), spread)[0:1]
    dsk3 = split3(hdot(jnp.broadcast_to(dskip_r[...], (8, HEADS)), spread), lane8)
    for g in range(INNER // GW):
        cols = pl.ds(g * GW, GW)
        head = (iota((128, GW), 1) + g * GW) >> 6
        row = iota((128, GW), 0)
        e4_v[:, cols] = (((row & 31) == head) & (row < 96)).astype(F32).astype(BF16)
        dsk_v[:, cols] = dot(dsk3, e4_v[:, cols])
    bd_v[...] = ((iota((GW, GW), 0) >> 6) == (iota((GW, GW), 1) >> 6)).astype(F32).astype(BF16)
    for h in range(QH):
        qz_v[h] = jnp.zeros((2 * HD, TOK), BF16)

    @pl.when(me == 0)
    def _():
        for s in range(NSEQ):
            for ch in range(NCH):
                hin_v[s, ch] = jnp.zeros((NST, CHW), F32)

    def norm_rows(start, count):
        def body(step, carry):
            rows = pl.ds(pl.multiple_of(start + step * 128, 128), 128)
            vals = x_v[rows, :].astype(F32)
            scale = lax.rsqrt(jnp.mean(vals * vals, axis=-1, keepdims=True) + EPS)
            u_v[rows, :] = (x_v[rows, :].astype(F32) * scale).astype(BF16)
            return carry
        lax.fori_loop(0, count // 128, body, 0)

    copies['x'].wait()
    norm_rows(0, ROWS)
    copies['wt'].wait()
    copies['wx0'].wait()

    tail = dot_t(u_v[...], wt_v[...])
    b_v[...] = tail[:, :NST].astype(BF16)
    c_v[...] = tail[:, NST:2 * NST].astype(BF16)
    r_bf = tail[:, 2 * NST:].astype(BF16)
    spread_bf = spread.astype(BF16)
    tri = (iota((TOK, TOK), 0) >= iota((TOK, TOK), 1)) & ((iota((TOK, TOK), 0) >> 6) == (iota((TOK, TOK), 1) >> 6))
    tri = tri.astype(F32)
    lane = iota((TOK, 128), 1)
    for s in range(NSEQ):
        pre = dot(r_bf[s * TOK:(s + 1) * TOK], spread_bf) + bias3
        dt = jnp.maximum(pre, 0.0) + jnp.log1p(jnp.exp(-jnp.abs(pre)))
        cum = hdot(tri, dt * aneg3)
        csp_v[s * TOK:(s + 1) * TOK, :] = split3(cum, lane)
        dsp_v[s * TOK:(s + 1) * TOK, :] = split3(dt, lane)

    def proj_x(ch):
        cols = pl.ds(ch * CHW, CHW)
        xs_v[:, cols] = dot_t(u_v[...], wx_v[cols, :]).astype(BF16)

    def head_spread(ch):
        cols = pl.ds(ch * CHW, CHW)
        ec_v[:, cols] = dot(csp_v[...], e4_v[:, cols])
        de_v[:, cols] = dot(dsp_v[...], e4_v[:, cols])

    t_idx = iota((BLK, GW), 0)
    s_idx = iota((BLK, GW), 1) & (BLK - 1)

    def ssd_blocks(s, ch):
        for b in range(NBLK):
            i = s * NBLK + b
            rows = pl.ds(i * BLK, BLK)
            bb = b_v[rows, :]
            sc4 = dot_t(c_v[rows, :], jnp.concatenate([bb] * 4, axis=0))
            bt = bb.astype(F32).T.astype(BF16)
            for half in range(CHW // GW):
                off = half * GW
                cols = pl.ds(ch * CHW + off, GW)
                ce = ec_v[rows, cols]
                de = de_v[rows, cols]
                crow = jnp.sum(jnp.where(t_idx == s_idx, ce, 0.0), axis=0, keepdims=True)
                drow = jnp.sum(jnp.where(t_idx == s_idx, de, 0.0), axis=0, keepdims=True)
                decay = jnp.exp(jnp.where(t_idx >= s_idx, ce - crow, -jnp.inf))
                mix = (sc4 * decay * drow).astype(BF16)
                xg = xs_v[rows, cols]
                xw = xg.astype(F32)
                xbd = jnp.concatenate([xg] * 4, axis=0) * bd_v[...]
                y_v[rows, cols] = dot(mix, xbd) + dsk_v[0:1, cols] * xw
                last = ce[BLK - 1:BLK, :]
                state = dot(bt, (xw * (jnp.exp(last - ce) * de)).astype(BF16))
                el = jnp.exp(last)
                bs_v[i, ch, :, off:off + GW] = state
                ec_v[rows, cols] = jnp.exp(ce)
                el_v[i * 8:i * 8 + 8, cols] = jnp.broadcast_to(el, (8, GW))
                if b == 0:
                    e_v[s, ch, :, off:off + GW] = state
                else:
                    e_v[s, ch, :, off:off + GW] = el * e_v[s, ch, :, off:off + GW] + state

    def st_copy(s, ch, dst):
        return pltpu.make_async_remote_copy(src_ref=e_v.at[s, ch], dst_ref=hin_v.at[s, ch], send_sem=st_ssem.at[s, ch], recv_sem=st_rsem.at[s, ch],
                                            device_id={'seq': dst}, device_id_type=pl.DeviceIdType.MESH)

    def chain(s, ch, dst):
        cols = pl.ds(ch * CHW, CHW)
        total = el_v[(s * NBLK) * 8:(s * NBLK) * 8 + 1, cols]
        for b in range(1, NBLK):
            total = total * el_v[(s * NBLK + b) * 8:(s * NBLK + b) * 8 + 1, cols]
        e_v[s, ch] = total * hin_v[s, ch] + e_v[s, ch]
        st_copy(s, ch, dst).start()

    def first_send(s, ch):
        @pl.when(me == 0)
        def _():
            st_copy(s, ch, 1).start()

    def relay(s, *chunks):
        @pl.when(me == 1)
        def _():
            for ch in chunks:
                st_copy(s, ch, 2).wait_recv()
                chain(s, ch, 2)

    proj_x(0)
    head_spread(0)
    ssd_blocks(0, 0)
    pl.semaphore_wait(barrier, 3)
    first_send(0, 0)
    copies['wx1'].wait()
    load('wout', wout_h, wout_v, 6)
    load('up', up1_h, up_v, 7)
    proj_x(1)
    head_spread(1)
    ssd_blocks(0, 1)
    first_send(0, 1)
    relay(0, 0)
    copies['wx2'].wait()
    proj_x(2)
    head_spread(2)
    ssd_blocks(0, 2)
    first_send(0, 2)
    relay(0, 1)
    load('down', down1_h, down_v, 8)
    load('wq', wq_h, wqkv_v.at[pl.ds(0, QH * HD), :], 9)
    load('wkv', wkv_h, wqkv_v.at[pl.ds(QH * HD, 256), :], 10)
    load('wo', wo_h, wo_v, 11)
    tab = pl.ds(pl.multiple_of(me * TOK, TOK), TOK)
    load('cos', cos_h.at[:, tab], cos_v, 12)
    load('sin', sin_h.at[:, tab], sin_v, 13)
    ssd_blocks(1, 0)
    first_send(1, 0)
    relay(0, 2)
    ssd_blocks(1, 1)
    first_send(1, 1)
    ssd_blocks(1, 2)
    first_send(1, 2)
    relay(1, 0, 1)
    copies['wz'].wait()
    for ch in range(NCH):
        cols = pl.ds(ch * CHW, CHW)
        z_v[:, cols] = dot_t(u_v[...], wz_v[cols, :]).astype(BF16)
    relay(1, 2)

    def ssd_finish(s):
        @pl.when(me == 2)
        def _():
            for ch in range(NCH):
                st_copy(s, ch, 3).wait_recv()
                chain(s, ch, 3)

        @pl.when(me == 3)
        def _():
            for ch in range(NCH):
                st_copy(s, ch, 3).wait_recv()

        for ch in range(NCH):
            cols = pl.ds(ch * CHW, CHW)
            for b in range(NBLK):
                i = s * NBLK + b
                rows = pl.ds(i * BLK, BLK)
                held = hin_v[s, ch]
                y_v[rows, cols] = y_v[rows, cols] + ec_v[rows, cols] * dot(c_v[rows, :], held.astype(BF16))
                if b < NBLK - 1:
                    hin_v[s, ch] = el_v[i * 8:i * 8 + 1, cols] * held + bs_v[i, ch]

        def gate(b, carry):
            rows = pl.ds(pl.multiple_of(s * TOK + b * BLK, BLK), BLK)
            ssq = jnp.zeros((BLK, 1), F32)
            for ch in range(NCH):
                yv = y_v[rows, ch * CHW:(ch + 1) * CHW]
                ssq = ssq + jnp.sum(yv * yv, axis=-1, keepdims=True)
            scale = lax.rsqrt(ssq * (1.0 / INNER) + EPS)
            for ch in range(NCH):
                cols = pl.ds(ch * CHW, CHW)
                xs_v[rows, cols] = (y_v[rows, cols] * scale * silu(z_v[rows, cols].astype(F32))).astype(BF16)
            return carry
        lax.fori_loop(0, NBLK, gate, 0, unroll=2)

        rows = pl.ds(s * TOK, TOK)
        for j in range(D // 512):
            cols = pl.ds(j * 512, 512)
            x_v[rows, cols] = (x_v[rows, cols].astype(F32) + dot(xs_v[rows, :], wout_v[:, cols])).astype(BF16)

    def mlp_up(start, count, width, per_step):
        rows = pl.ds(start, count)

        def body(j, carry):
            for k in range(per_step):
                c0 = pl.multiple_of((j * per_step + k) * width, width)
                gate = dot(u_v[rows, :], up_v[:, pl.ds(c0, width)])
                up = dot(u_v[rows, :], up_v[:, pl.ds(FF + c0, width)])
                act_v[rows, pl.ds(c0, width)] = (silu(gate) * up).astype(BF16)
            return carry
        lax.fori_loop(0, FF // (width * per_step), body, 0)

    def mlp_down(start, count, width, out_copy=None):
        rows = pl.ds(start, count)
        for j in range(D // width):
            cols = pl.ds(j * width, width)
            x_v[rows, cols] = (x_v[rows, cols].astype(F32) + dot(act_v[rows, :], down_v[:, cols])).astype(BF16)
            if out_copy is not None:
                out_copy(j).start()

    def k_copy(s, piece, slot, dst):
        return pltpu.make_async_remote_copy(src_ref=kv_v.at[s, piece], dst_ref=kv_v.at[s, piece], send_sem=k_ssem.at[s, slot], recv_sem=k_rsem.at[s, piece],
                                            device_id={'seq': dst}, device_id_type=pl.DeviceIdType.MESH)

    def v_copy(s, piece, slot, dst):
        return pltpu.make_async_remote_copy(src_ref=vt_v.at[s, piece], dst_ref=vt_v.at[s, piece], send_sem=v_ssem.at[s, slot], recv_sem=v_rsem.at[s, piece],
                                            device_id={'seq': dst}, device_id_type=pl.DeviceIdType.MESH)

    def kv_send(s, piece, slot, dst):
        k_copy(s, piece, slot, dst).start()
        v_copy(s, piece, slot, dst).start()

    def kv_wait(s, piece):
        k_copy(s, piece, 0, 0).wait_recv()
        v_copy(s, piece, 0, 0).wait_recv()

    def kv_sent(s, piece, slot, dst):
        k_copy(s, piece, slot, dst).wait_send()
        v_copy(s, piece, slot, dst).wait_send()

    def rope(first, second):
        cos = cos_v[...]
        sin = sin_v[...]
        return first * cos - second * sin, second * cos + first * sin

    def qkv(s):
        rows = pl.ds(s * TOK, TOK)
        norm_rows(s * TOK, TOK)
        kv_t = dot_t(wqkv_v[QH * HD:, :], u_v[rows, :])
        parts = []
        for g in range(2):
            parts.extend(rope(kv_t[g * HD:g * HD + 32], kv_t[g * HD + 32:g * HD + HD]))
        kv_v[s, me] = jnp.concatenate(parts, axis=0).T.astype(BF16)
        vt_v[s, me] = kv_t[2 * HD:].astype(BF16)
        q_t = dot_t(wqkv_v[:QH * HD, :], u_v[rows, :])
        for h in range(QH):
            top = (h // 4) * HD
            lo, hi = rope(q_t[h * HD:h * HD + 32], q_t[h * HD + 32:h * HD + HD])
            qz_v[h, top:top + 32, :] = (lo * 0.125).astype(BF16)
            qz_v[h, top + 32:top + HD, :] = (hi * 0.125).astype(BF16)

        @pl.when(me == 0)
        def _():
            kv_send(s, 0, 0, 1)
            kv_send(s, 0, 1, 2)

        @pl.when(me == 1)
        def _():
            kv_send(s, 1, 0, 3)

        @pl.when(me == 2)
        def _():
            kv_send(s, 2, 0, 3)
            kv_wait(s, 0)
            kv_send(s, 0, 1, 3)

        @pl.when(me == 3)
        def _():
            kv_wait(s, 1)
            kv_send(s, 1, 0, 2)

    def attend(s, piece, first):
        causal = iota((TOK, TOK), 0) <= iota((TOK, TOK), 1)

        def score(h):
            sc_v[h] = dot(kv_v[s, piece], qz_v[h])

        def soft(h):
            sc = sc_v[h]
            if first:
                sc = jnp.where(causal, sc, -jnp.inf)
                top = jnp.max(sc, axis=0, keepdims=True)
                prob = jnp.exp(sc - top)
                l_v[h] = jnp.sum(prob, axis=0, keepdims=True)
                fix = None
            else:
                old = m_v[h]
                top = jnp.maximum(old, jnp.max(sc, axis=0, keepdims=True))
                fix = jnp.exp(old - top)
                prob = jnp.exp(sc - top)
                l_v[h] = l_v[h] * fix + jnp.sum(prob, axis=0, keepdims=True)
            m_v[h] = top
            pr_v[h] = prob.astype(BF16)
            return fix

        def mix(h, fix):
            g = h // 4
            out = dot(vt_v[s, piece, g * HD:(g + 1) * HD, :], pr_v[h])
            acc_v[h] = out if first else acc_v[h] * fix + out

        score(0)
        score(1)
        fixes = {}
        for h in range(QH):
            if h + 2 < QH:
                score(h + 2)
            fixes[h] = soft(h)
            if h >= 1:
                mix(h - 1, fixes[h - 1])
        mix(QH - 1, fixes[QH - 1])

    def attention(s):
        attend(s, me, True)

        def older(piece, carry):
            early = ((me == 2) & (piece == 0)) | ((me == 3) & (piece == 1))

            @pl.when(jnp.logical_not(early))
            def _():
                kv_wait(s, piece)
            attend(s, piece, False)
            return carry
        lax.fori_loop(0, me, older, 0)
        rows = pl.ds(s * TOK, TOK)
        for pair in range(QH // 2):
            top = acc_v[2 * pair] / l_v[2 * pair]
            bot = acc_v[2 * pair + 1] / l_v[2 * pair + 1]
            att_v[:, pair * 128:(pair + 1) * 128] = jnp.concatenate([top, bot], axis=0).T.astype(BF16)
        for j in range(D // 512):
            cols = pl.ds(j * 512, 512)
            x_v[rows, cols] = (x_v[rows, cols].astype(F32) + dot(att_v[...], wo_v[:, cols])).astype(BF16)

    copies['wout'].wait()
    ssd_finish(0)
    norm_rows(0, TOK)
    copies['up'].wait()
    mlp_up(0, TOK, 512, 2)
    copies['down'].wait()
    mlp_down(0, TOK, 512)
    for name in ('wq', 'wkv', 'wo', 'cos', 'sin'):
        copies[name].wait()
    qkv(0)
    attention(0)
    ssd_finish(1)
    norm_rows(TOK, TOK)
    mlp_up(TOK, TOK, 512, 2)
    load('up', up2_h, up_v, 7)
    mlp_down(TOK, TOK, 512)
    load('down', down2_h, down_v, 8)
    qkv(1)
    attention(1)
    norm_rows(0, ROWS)
    copies['up'].wait()
    mlp_up(0, ROWS, 256, 2)
    copies['down'].wait()

    def out_copy(j):
        cols = pl.ds(j * 256, 256)
        return pltpu.make_async_copy(x_v.at[:, cols], out_h.at[:, cols], osem.at[j])
    mlp_down(0, ROWS, 256, out_copy)

    @pl.when(me < 3)
    def _():
        for s in range(NSEQ):
            for ch in range(NCH):
                st_copy(s, ch, 0).wait_send()
    for s in range(NSEQ):
        kv_sent(s, 0, 0, 0)

        @pl.when((me == 0) | (me == 2))
        def _():
            kv_sent(s, 0, 1, 0)
    for j in range(D // 256):
        out_copy(j).wait()


def rope_tables(seq_len):
    inv = (np.float32(ROPE_BASE) ** (-(np.arange(32, dtype=np.float32) * np.float32(2.0) / np.float32(HD)))).astype(np.float32)
    ang = (inv[:, None] * np.arange(seq_len, dtype=np.float32)[None, :]).astype(np.float32).astype(np.float64)
    return np.cos(ang).astype(np.float32), np.sin(ang).astype(np.float32)


def solution(mesh):
    n_dev = mesh.shape['seq']
    cos_t, sin_t = rope_tables(n_dev * TOK)
    any_spec = pl.BlockSpec(memory_space=pl.ANY)
    vm_spec = pl.BlockSpec(memory_space=pltpu.VMEM)
    vm = pltpu.VMEM
    call = pl.pallas_call(
        kernel,
        out_shape=jax.ShapeDtypeStruct((ROWS, D), BF16),
        in_specs=[any_spec, any_spec, vm_spec, vm_spec, vm_spec] + [any_spec] * 10,
        out_specs=any_spec,
        scratch_shapes=[
            vm((ROWS, D), BF16), vm((ROWS, D), BF16), vm((INNER, D), BF16), vm((INNER, D), BF16), vm((2 * NST + HEADS, D), BF16),
            vm((INNER, D), BF16), vm((D, 2 * FF), BF16), vm((FF, D), BF16), vm((QH * HD + 256, D), BF16), vm((QH * HD, D), BF16),
            vm((32, TOK), F32), vm((32, TOK), F32),
            vm((ROWS, INNER), BF16), vm((ROWS, INNER), BF16), vm((ROWS, NST), BF16), vm((ROWS, NST), BF16),
            vm((ROWS, 128), BF16), vm((ROWS, 128), BF16), vm((128, INNER), BF16), vm((GW, GW), BF16),
            vm((ROWS, INNER), F32), vm((ROWS, INNER), F32), vm((ROWS, INNER), F32), vm((NSEQ * NBLK * 8, INNER), F32), vm((8, INNER), F32),
            vm((NSEQ * NBLK, NCH, NST, CHW), F32), vm((NSEQ, NCH, NST, CHW), F32), vm((NSEQ, NCH, NST, CHW), F32), vm((ROWS, FF), BF16),
            vm((QH, 2 * HD, TOK), BF16), vm((NSEQ, 4, TOK, 128), BF16), vm((NSEQ, 4, 128, TOK), BF16),
            vm((QH, 1, TOK), F32), vm((QH, 1, TOK), F32), vm((QH, HD, TOK), F32), vm((TOK, QH * HD), BF16),
            vm((QH, TOK, TOK), F32), vm((QH, TOK, TOK), BF16),
            pltpu.SemaphoreType.DMA((14,)), pltpu.SemaphoreType.DMA((4,)), pltpu.SemaphoreType.DMA((NSEQ, NCH)), pltpu.SemaphoreType.DMA((NSEQ, NCH)),
            pltpu.SemaphoreType.DMA((NSEQ, 2)), pltpu.SemaphoreType.DMA((NSEQ, 4)), pltpu.SemaphoreType.DMA((NSEQ, 2)), pltpu.SemaphoreType.DMA((NSEQ, 4)),
        ],
        compiler_params=pltpu.CompilerParams(collective_id=0, has_side_effects=True, vmem_limit_bytes=67_000_000),
        name='layer_stack',
    )

    def local_fn(x_loc, w_in, dt_bias, a_neg, d_skip, w_out, w_up1, w_down1, w_q, w_kv, w_o, w_up2, w_down2):
        w_q_t = w_q.transpose(1, 2, 0).reshape(QH * HD, D)
        w_kv_t = w_kv.transpose(1, 2, 3, 0).reshape(256, D)
        out = call(x_loc.reshape(ROWS, D), w_in.T, dt_bias.reshape(1, HEADS), a_neg.reshape(1, HEADS), d_skip.reshape(1, HEADS), w_out, w_up1, w_down1,
                   w_q_t, w_kv_t, w_o.reshape(QH * HD, D), w_up2, w_down2, jnp.asarray(cos_t), jnp.asarray(sin_t))
        return out.reshape(x_loc.shape)

    seq_spec = P('data', 'seq', None)
    return jax.shard_map(local_fn, mesh=mesh, in_specs=(seq_spec,) + (P(),) * 12, out_specs=seq_spec, check_vma=False)
```

time: 92.8 us -> 56.7 us (0.61)
  Pallas kernels: 76 us -> 54.2 us
  local copies, waits for them, and re-layouts: 16.3 us -> 2.26 us
    pallas_call x1, Pallas kernels: 76 us -> 54.2 us  [local_fn(): call(x_loc.reshape(ROWS, D), w_in.T, dt_bias.reshape(1, HEADS), a_neg.res...]
    unnamed x2 -> x1, local copies, waits for them, and re-layouts: 11.9 us -> 2.26 us
    reshape x2 -> x0, local copies, waits for them, and re-layouts: 4.36 us -> none  [the longest x1 2.27 us: local_fn(): w_q.reshape(D, QH * HD)]
where the time goes in v2:
time: 56.7 us; the launch traced here: 56.5 us
  Pallas kernels  54.2 us (96%)
  local copies, waits for them, and re-layouts  2.26 us (4%)
    pallas_call x1, Pallas kernels, local_fn(): call(x_loc.reshape(ROWS, D), w_in.T, dt_bias.reshape(1, HEADS), a_neg.res...  54.2 us
    unnamed x1, local copies, waits for them, and re-layouts  2.26 us

profile of v2, /device:TPU:7, one launch (start us, length us, event | category | flops | bytes accessed | tf_op | source)
XLA Modules:
  0.0 56.5 jit_solution(13745469392912959218)
XLA Ops:
  0.0 54.2 %layer_stack.1 = bf16[512,1024]{1,0:T(8,128)(2,1)} custom-call(bf16[512,1024]{1,0:T(8,128)(2,1)} %bitcast.15, bf16[3352,1024]{1,0:T(8,128)(2,1)} %bitcast.13, f32[1,24]{1,0:T(1,128)} %bitcast.19, f32[1,24]{1,0:T(1,128)} %bitcast.20, f32[1,24]{1,0:T(1,128)} %bitcast.21, bf16[1536,1024]{1,0:T(8,128)(2,1)} %wout_h.1, bf16[1024,4096]{1,0:T(8,128)(2,1)} %up1_h.1, ...), custom_call_target="tpu_custom_call" | custom-call | tf_op jit(solution)/shard_map/layer_stack/pallas_call | solution.py:503
  54.3 2.3 %copy.17 = bf16[2,256,1024]{2,1,0:T(8,128)(2,1)} copy(bf16[2,256,1024]{2,1,0:T(8,128)(2,1)} %bitcast.14) | data formatting | bytes 2097152

commit v3 on v2

--- a/solution.py
+++ b/solution.py
@@ -21,7 +21,7 @@
 HEADS = 24
 NST = 128
 FF = 2048
-NCH = 3
+NCH = 6
 CHW = INNER // NCH
 GW = 256
 HD = 64
@@ -59,7 +59,7 @@
 def kernel(x_h, win_h, bias_r, aneg_r, dskip_r, wout_h, up1_h, down1_h, wq_h, wkv_h, wo_h, up2_h, down2_h, cos_h, sin_h, out_h,
            x_v, u_v, wx_v, wz_v, wt_v, wout_v, up_v, down_v, wqkv_v, wo_v, cos_v, sin_v,
            xs_v, z_v, b_v, c_v, csp_v, dsp_v, e4_v, bd_v, y_v, ec_v, de_v, el_v, dsk_v, bs_v, e_v, hin_v, act_v,
-           qz_v, kv_v, vt_v, m_v, l_v, acc_v, att_v, sc_v, pr_v,
+           qz_v, kv_v, vt_v, m_v, l_v, acc_v, att_v, sc_v, pr_v, sc4_v, bt_v,
            lsem, osem, st_ssem, st_rsem, k_ssem, k_rsem, v_ssem, v_rsem):
     me = lax.axis_index('seq')
     copies = {}
@@ -70,8 +70,8 @@
 
     load('x', x_h, x_v, 0)
     load('wt', win_h.at[pl.ds(2 * INNER, 2 * NST + HEADS), :], wt_v, 1)
-    for ch in range(NCH):
-        load('wx%d' % ch, win_h.at[pl.ds(ch * CHW, CHW), :], wx_v.at[pl.ds(ch * CHW, CHW), :], 2 + ch)
+    load('wx0', win_h.at[pl.ds(0, CHW), :], wx_v.at[pl.ds(0, CHW), :], 2)
+    load('wx1', win_h.at[pl.ds(CHW, INNER - CHW), :], wx_v.at[pl.ds(CHW, INNER - CHW), :], 3)
     load('wz', win_h.at[pl.ds(INNER, INNER), :], wz_v, 5)
 
     barrier = pltpu.get_barrier_semaphore()
@@ -107,27 +107,44 @@
             scale = lax.rsqrt(jnp.mean(vals * vals, axis=-1, keepdims=True) + EPS)
             u_v[rows, :] = (x_v[rows, :].astype(F32) * scale).astype(BF16)
             return carry
-        lax.fori_loop(0, count // 128, body, 0)
+        lax.fori_loop(0, count // 128, body, 0, unroll=2)
 
     copies['x'].wait()
     norm_rows(0, ROWS)
     copies['wt'].wait()
     copies['wx0'].wait()
 
-    tail = dot_t(u_v[...], wt_v[...])
-    b_v[...] = tail[:, :NST].astype(BF16)
-    c_v[...] = tail[:, NST:2 * NST].astype(BF16)
-    r_bf = tail[:, 2 * NST:].astype(BF16)
     spread_bf = spread.astype(BF16)
     tri = (iota((TOK, TOK), 0) >= iota((TOK, TOK), 1)) & ((iota((TOK, TOK), 0) >> 6) == (iota((TOK, TOK), 1) >> 6))
-    tri = tri.astype(F32)
+    tri = tri.astype(F32).astype(BF16)
     lane = iota((TOK, 128), 1)
-    for s in range(NSEQ):
-        pre = dot(r_bf[s * TOK:(s + 1) * TOK], spread_bf) + bias3
+
+    def decay_sums(s):
+        rows = pl.ds(s * TOK, TOK)
+        r_bf = dot_t(u_v[rows, :], wt_v[2 * NST:, :]).astype(BF16)
+        pre = dot(r_bf, spread_bf) + bias3
         dt = jnp.maximum(pre, 0.0) + jnp.log1p(jnp.exp(-jnp.abs(pre)))
-        cum = hdot(tri, dt * aneg3)
-        csp_v[s * TOK:(s + 1) * TOK, :] = split3(cum, lane)
-        dsp_v[s * TOK:(s + 1) * TOK, :] = split3(dt, lane)
+        part = dot(tri, split3(dt * aneg3, lane))
+        cum = (part + pltpu.roll(part, 96, 1)) + pltpu.roll(part, 64, 1)
+        cum = jnp.where(lane < 32, cum, jnp.where(lane < 64, pltpu.roll(cum, 32, 1), pltpu.roll(cum, 64, 1)))
+        csp_v[rows, :] = split3(cum, lane)
+        dsp_v[rows, :] = split3(dt, lane)
+
+    def block_scores(s):
+        rows = pl.ds(s * TOK, TOK)
+        bc = dot_t(u_v[rows, :], wt_v[:2 * NST, :])
+        b_v[rows, :] = bc[:, :NST].astype(BF16)
+        c_v[rows, :] = bc[:, NST:].astype(BF16)
+        for b in range(NBLK):
+            i = s * NBLK + b
+            blk = pl.ds(i * BLK, BLK)
+            bb = b_v[blk, :]
+            sc4_v[blk, :] = dot_t(c_v[blk, :], jnp.concatenate([bb] * 4, axis=0))
+            bt_v[i] = bb.astype(F32).T.astype(BF16)
+
+    decay_sums(0)
+    decay_sums(1)
+    block_scores(0)
 
     def proj_x(ch):
         cols = pl.ds(ch * CHW, CHW)
@@ -145,9 +162,6 @@
         for b in range(NBLK):
             i = s * NBLK + b
             rows = pl.ds(i * BLK, BLK)
-            bb = b_v[rows, :]
-            sc4 = dot_t(c_v[rows, :], jnp.concatenate([bb] * 4, axis=0))
-            bt = bb.astype(F32).T.astype(BF16)
             for half in range(CHW // GW):
                 off = half * GW
                 cols = pl.ds(ch * CHW + off, GW)
@@ -156,21 +170,22 @@
                 crow = jnp.sum(jnp.where(t_idx == s_idx, ce, 0.0), axis=0, keepdims=True)
                 drow = jnp.sum(jnp.where(t_idx == s_idx, de, 0.0), axis=0, keepdims=True)
                 decay = jnp.exp(jnp.where(t_idx >= s_idx, ce - crow, -jnp.inf))
-                mix = (sc4 * decay * drow).astype(BF16)
+                mix = (sc4_v[rows, :] * decay * drow).astype(BF16)
                 xg = xs_v[rows, cols]
                 xw = xg.astype(F32)
                 xbd = jnp.concatenate([xg] * 4, axis=0) * bd_v[...]
                 y_v[rows, cols] = dot(mix, xbd) + dsk_v[0:1, cols] * xw
                 last = ce[BLK - 1:BLK, :]
-                state = dot(bt, (xw * (jnp.exp(last - ce) * de)).astype(BF16))
-                el = jnp.exp(last)
+                state = dot(bt_v[i], (xw * (jnp.exp(last - ce) * de)).astype(BF16))
                 bs_v[i, ch, :, off:off + GW] = state
                 ec_v[rows, cols] = jnp.exp(ce)
-                el_v[i * 8:i * 8 + 8, cols] = jnp.broadcast_to(el, (8, GW))
-                if b == 0:
-                    e_v[s, ch, :, off:off + GW] = state
-                else:
-                    e_v[s, ch, :, off:off + GW] = el * e_v[s, ch, :, off:off + GW] + state
+                el_v[i * 8:i * 8 + 8, cols] = jnp.broadcast_to(jnp.exp(last), (8, GW))
+        cols = pl.ds(ch * CHW, CHW)
+        end = bs_v[s * NBLK, ch]
+        for b in range(1, NBLK):
+            i = s * NBLK + b
+            end = el_v[i * 8:i * 8 + 1, cols] * end + bs_v[i, ch]
+        e_v[s, ch] = end
 
     def st_copy(s, ch, dst):
         return pltpu.make_async_remote_copy(src_ref=e_v.at[s, ch], dst_ref=hin_v.at[s, ch], send_sem=st_ssem.at[s, ch], recv_sem=st_rsem.at[s, ch],
@@ -196,25 +211,35 @@
                 st_copy(s, ch, 2).wait_recv()
                 chain(s, ch, 2)
 
+    def proj_z(ch):
+        cols = pl.ds(ch * CHW, CHW)
+        z_v[:, cols] = dot_t(u_v[...], wz_v[cols, :]).astype(BF16)
+
     proj_x(0)
     head_spread(0)
     ssd_blocks(0, 0)
-    pl.semaphore_wait(barrier, 3)
-    first_send(0, 0)
+    @pl.when(me == 0)
+    def _():
+        pl.semaphore_wait(barrier, 3)
+        st_copy(0, 0, 1).start()
+
+    @pl.when(me != 0)
+    def _():
+        pl.semaphore_wait(barrier, 3)
+
     copies['wx1'].wait()
     load('wout', wout_h, wout_v, 6)
     load('up', up1_h, up_v, 7)
     proj_x(1)
     head_spread(1)
-    ssd_blocks(0, 1)
-    first_send(0, 1)
-    relay(0, 0)
-    copies['wx2'].wait()
-    proj_x(2)
-    head_spread(2)
-    ssd_blocks(0, 2)
-    first_send(0, 2)
-    relay(0, 1)
+    block_scores(1)
+    for ch in range(1, NCH):
+        if ch + 1 < NCH:
+            proj_x(ch + 1)
+            head_spread(ch + 1)
+        ssd_blocks(0, ch)
+        first_send(0, ch)
+        relay(0, ch - 1)
     load('down', down1_h, down_v, 8)
     load('wq', wq_h, wqkv_v.at[pl.ds(0, QH * HD), :], 9)
     load('wkv', wkv_h, wqkv_v.at[pl.ds(QH * HD, 256), :], 10)
@@ -222,41 +247,39 @@
     tab = pl.ds(pl.multiple_of(me * TOK, TOK), TOK)
     load('cos', cos_h.at[:, tab], cos_v, 12)
     load('sin', sin_h.at[:, tab], sin_v, 13)
-    ssd_blocks(1, 0)
-    first_send(1, 0)
-    relay(0, 2)
-    ssd_blocks(1, 1)
-    first_send(1, 1)
-    ssd_blocks(1, 2)
-    first_send(1, 2)
-    relay(1, 0, 1)
     copies['wz'].wait()
     for ch in range(NCH):
-        cols = pl.ds(ch * CHW, CHW)
-        z_v[:, cols] = dot_t(u_v[...], wz_v[cols, :]).astype(BF16)
-    relay(1, 2)
+        proj_z(ch)
+        ssd_blocks(1, ch)
+        first_send(1, ch)
+        if ch == 0:
+            relay(0, NCH - 1)
+        elif ch >= 2:
+            relay(1, ch - 2)
+    relay(1, NCH - 2, NCH - 1)
 
     def ssd_finish(s):
-        @pl.when(me == 2)
-        def _():
-            for ch in range(NCH):
-                st_copy(s, ch, 3).wait_recv()
-                chain(s, ch, 3)
-
-        @pl.when(me == 3)
-        def _():
-            for ch in range(NCH):
-                st_copy(s, ch, 3).wait_recv()
-
-        for ch in range(NCH):
-            cols = pl.ds(ch * CHW, CHW)
-            for b in range(NBLK):
-                i = s * NBLK + b
-                rows = pl.ds(i * BLK, BLK)
+        for group in (range(NCH // 2), range(NCH // 2, NCH)):
+            @pl.when(me == 2)
+            def _(group=group):
+                for ch in group:
+                    st_copy(s, ch, 3).wait_recv()
+                    chain(s, ch, 3)
+
+            @pl.when(me == 3)
+            def _(group=group):
+                for ch in group:
+                    st_copy(s, ch, 3).wait_recv()
+
+            for ch in group:
+                cols = pl.ds(ch * CHW, CHW)
                 held = hin_v[s, ch]
-                y_v[rows, cols] = y_v[rows, cols] + ec_v[rows, cols] * dot(c_v[rows, :], held.astype(BF16))
-                if b < NBLK - 1:
-                    hin_v[s, ch] = el_v[i * 8:i * 8 + 1, cols] * held + bs_v[i, ch]
+                for b in range(NBLK):
+                    i = s * NBLK + b
+                    rows = pl.ds(i * BLK, BLK)
+                    y_v[rows, cols] = y_v[rows, cols] + ec_v[rows, cols] * dot(c_v[rows, :], held.astype(BF16))
+                    if b < NBLK - 1:
+                        held = el_v[i * 8:i * 8 + 1, cols] * held + bs_v[i, ch]
 
         def gate(b, carry):
             rows = pl.ds(pl.multiple_of(s * TOK + b * BLK, BLK), BLK)
@@ -276,17 +299,12 @@
             cols = pl.ds(j * 512, 512)
             x_v[rows, cols] = (x_v[rows, cols].astype(F32) + dot(xs_v[rows, :], wout_v[:, cols])).astype(BF16)
 
-    def mlp_up(start, count, width, per_step):
+    def mlp_up(start, count):
         rows = pl.ds(start, count)
-
-        def body(j, carry):
-            for k in range(per_step):
-                c0 = pl.multiple_of((j * per_step + k) * width, width)
-                gate = dot(u_v[rows, :], up_v[:, pl.ds(c0, width)])
-                up = dot(u_v[rows, :], up_v[:, pl.ds(FF + c0, width)])
-                act_v[rows, pl.ds(c0, width)] = (silu(gate) * up).astype(BF16)
-            return carry
-        lax.fori_loop(0, FF // (width * per_step), body, 0)
+        for j in range(FF // 256):
+            gate = dot(u_v[rows, :], up_v[:, j * 256:(j + 1) * 256])
+            up = dot(u_v[rows, :], up_v[:, FF + j * 256:FF + (j + 1) * 256])
+            act_v[rows, j * 256:(j + 1) * 256] = (silu(gate) * up).astype(BF16)
 
     def mlp_down(start, count, width, out_copy=None):
         rows = pl.ds(start, count)
@@ -364,21 +382,27 @@
             sc_v[h] = dot(kv_v[s, piece], qz_v[h])
 
         def soft(h):
-            sc = sc_v[h]
-            if first:
-                sc = jnp.where(causal, sc, -jnp.inf)
-                top = jnp.max(sc, axis=0, keepdims=True)
-                prob = jnp.exp(sc - top)
-                l_v[h] = jnp.sum(prob, axis=0, keepdims=True)
-                fix = None
-            else:
+            pieces = range(TOK // 64)
+
+            def load_scores(r):
+                sc = sc_v[h, r * 64:(r + 1) * 64, :]
+                return jnp.where(causal[r * 64:(r + 1) * 64], sc, -jnp.inf) if first else sc
+
+            top = jnp.concatenate([jnp.max(load_scores(r).reshape(8, 8, TOK), axis=0) for r in pieces], axis=0)
+            top = jnp.max(top, axis=0, keepdims=True)
+            fix = None
+            if not first:
                 old = m_v[h]
-                top = jnp.maximum(old, jnp.max(sc, axis=0, keepdims=True))
+                top = jnp.maximum(old, top)
                 fix = jnp.exp(old - top)
-                prob = jnp.exp(sc - top)
-                l_v[h] = l_v[h] * fix + jnp.sum(prob, axis=0, keepdims=True)
+            total = jnp.zeros((8, TOK), F32)
+            for r in pieces:
+                prob = jnp.exp(load_scores(r) - top)
+                total = total + jnp.sum(prob.reshape(8, 8, TOK), axis=0)
+                pr_v[h, r * 64:(r + 1) * 64, :] = prob.astype(BF16)
+            total = jnp.sum(total, axis=0, keepdims=True)
+            l_v[h] = total if first else l_v[h] * fix + total
             m_v[h] = top
-            pr_v[h] = prob.astype(BF16)
             return fix
 
         def mix(h, fix):
@@ -422,7 +446,7 @@
     ssd_finish(0)
     norm_rows(0, TOK)
     copies['up'].wait()
-    mlp_up(0, TOK, 512, 2)
+    mlp_up(0, TOK)
     copies['down'].wait()
     mlp_down(0, TOK, 512)
     for name in ('wq', 'wkv', 'wo', 'cos', 'sin'):
@@ -431,7 +455,7 @@
     attention(0)
     ssd_finish(1)
     norm_rows(TOK, TOK)
-    mlp_up(TOK, TOK, 512, 2)
+    mlp_up(TOK, TOK)
     load('up', up2_h, up_v, 7)
     mlp_down(TOK, TOK, 512)
     load('down', down2_h, down_v, 8)
@@ -439,7 +463,7 @@
     attention(1)
     norm_rows(0, ROWS)
     copies['up'].wait()
-    mlp_up(0, ROWS, 256, 2)
+    mlp_up(0, ROWS)
     copies['down'].wait()
 
     def out_copy(j):
@@ -489,7 +513,7 @@
             vm((NSEQ * NBLK, NCH, NST, CHW), F32), vm((NSEQ, NCH, NST, CHW), F32), vm((NSEQ, NCH, NST, CHW), F32), vm((ROWS, FF), BF16),
             vm((QH, 2 * HD, TOK), BF16), vm((NSEQ, 4, TOK, 128), BF16), vm((NSEQ, 4, 128, TOK), BF16),
             vm((QH, 1, TOK), F32), vm((QH, 1, TOK), F32), vm((QH, HD, TOK), F32), vm((TOK, QH * HD), BF16),
-            vm((QH, TOK, TOK), F32), vm((QH, TOK, TOK), BF16),
+            vm((QH, TOK, TOK), F32), vm((QH, TOK, TOK), BF16), vm((ROWS, GW), F32), vm((NSEQ * NBLK, NST, BLK), BF16),
             pltpu.SemaphoreType.DMA((14,)), pltpu.SemaphoreType.DMA((4,)), pltpu.SemaphoreType.DMA((NSEQ, NCH)), pltpu.SemaphoreType.DMA((NSEQ, NCH)),
             pltpu.SemaphoreType.DMA((NSEQ, 2)), pltpu.SemaphoreType.DMA((NSEQ, 4)), pltpu.SemaphoreType.DMA((NSEQ, 2)), pltpu.SemaphoreType.DMA((NSEQ, 4)),
         ],

time: 56.7 us -> 54 us (0.952)
  Pallas kernels: 54.2 us -> 51.6 us
    pallas_call x1, Pallas kernels: 54.2 us -> 51.6 us  [local_fn(): call(x_loc.reshape(ROWS, D), w_in.T, dt_bias.reshape(1, HEADS), a_neg.res...]
where the time goes in v3:
time: 54 us; the launch traced here: 53.9 us
  Pallas kernels  51.6 us (96%)
  local copies, waits for them, and re-layouts  2.26 us (4%)
    pallas_call x1, Pallas kernels, local_fn(): call(x_loc.reshape(ROWS, D), w_in.T, dt_bias.reshape(1, HEADS), a_neg.res...  51.6 us
    unnamed x1, local copies, waits for them, and re-layouts  2.26 us

profile of v3, /device:TPU:7, one launch (start us, length us, event | category | flops | bytes accessed | tf_op | source)
XLA Modules:
  0.0 53.9 jit_solution(5036079257306964833)
XLA Ops:
  0.0 51.6 %layer_stack.1 = bf16[512,1024]{1,0:T(8,128)(2,1)} custom-call(bf16[512,1024]{1,0:T(8,128)(2,1)} %bitcast.15, bf16[3352,1024]{1,0:T(8,128)(2,1)} %bitcast.13, f32[1,24]{1,0:T(1,128)} %bitcast.19, f32[1,24]{1,0:T(1,128)} %bitcast.20, f32[1,24]{1,0:T(1,128)} %bitcast.21, bf16[1536,1024]{1,0:T(8,128)(2,1)} %wout_h.1, bf16[1024,4096]{1,0:T(8,128)(2,1)} %up1_h.1, ...), custom_call_target="tpu_custom_call" | custom-call | tf_op jit(solution)/shard_map/layer_stack/pallas_call | solution.py:527
  51.6 2.3 %copy.17 = bf16[2,256,1024]{2,1,0:T(8,128)(2,1)} copy(bf16[2,256,1024]{2,1,0:T(8,128)(2,1)} %bitcast.14) | data formatting | bytes 2097152

commit v4 on v3

--- a/solution.py
+++ b/solution.py
@@ -57,7 +57,7 @@
 
 
 def kernel(x_h, win_h, bias_r, aneg_r, dskip_r, wout_h, up1_h, down1_h, wq_h, wkv_h, wo_h, up2_h, down2_h, cos_h, sin_h, out_h,
-           x_v, u_v, wx_v, wz_v, wt_v, wout_v, up_v, down_v, wqkv_v, wo_v, cos_v, sin_v,
+           x_v, u_v, wx_v, wz_v, wt_v, wr_v, wout_v, up_v, down_v, wqkv_v, wo_v, cos_v, sin_v,
            xs_v, z_v, b_v, c_v, csp_v, dsp_v, e4_v, bd_v, y_v, ec_v, de_v, el_v, dsk_v, bs_v, e_v, hin_v, act_v,
            qz_v, kv_v, vt_v, m_v, l_v, acc_v, att_v, sc_v, pr_v, sc4_v, bt_v,
            lsem, osem, st_ssem, st_rsem, k_ssem, k_rsem, v_ssem, v_rsem):
@@ -68,9 +68,12 @@
         copies[name] = pltpu.make_async_copy(src, dst, lsem.at[idx])
         copies[name].start()
 
-    load('x', x_h, x_v, 0)
-    load('wt', win_h.at[pl.ds(2 * INNER, 2 * NST + HEADS), :], wt_v, 1)
+    load('xa', x_h.at[pl.ds(0, TOK), :], x_v.at[pl.ds(0, TOK), :], 0)
+    for k in range(3):
+        load('wr%d' % k, win_h.at[pl.ds(2 * INNER + 2 * NST, HEADS), :], wr_v.at[pl.ds(32 * k, HEADS), :], 14 + k)
+    load('wt', win_h.at[pl.ds(2 * INNER, 2 * NST), :], wt_v, 1)
     load('wx0', win_h.at[pl.ds(0, CHW), :], wx_v.at[pl.ds(0, CHW), :], 2)
+    load('xb', x_h.at[pl.ds(TOK, TOK), :], x_v.at[pl.ds(TOK, TOK), :], 4)
     load('wx1', win_h.at[pl.ds(CHW, INNER - CHW), :], wx_v.at[pl.ds(CHW, INNER - CHW), :], 3)
     load('wz', win_h.at[pl.ds(INNER, INNER), :], wz_v, 5)
 
@@ -91,6 +94,8 @@
         e4_v[:, cols] = (((row & 31) == head) & (row < 96)).astype(F32).astype(BF16)
         dsk_v[:, cols] = dot(dsk3, e4_v[:, cols])
     bd_v[...] = ((iota((GW, GW), 0) >> 6) == (iota((GW, GW), 1) >> 6)).astype(F32).astype(BF16)
+    for lo, hi in ((24, 32), (56, 64), (88, 128)):
+        wr_v[lo:hi, :] = jnp.zeros((hi - lo, D), BF16)
     for h in range(QH):
         qz_v[h] = jnp.zeros((2 * HD, TOK), BF16)
 
@@ -109,20 +114,20 @@
             return carry
         lax.fori_loop(0, count // 128, body, 0, unroll=2)
 
-    copies['x'].wait()
-    norm_rows(0, ROWS)
+    copies['xa'].wait()
+    norm_rows(0, TOK)
+    for k in range(3):
+        copies['wr%d' % k].wait()
     copies['wt'].wait()
     copies['wx0'].wait()
 
-    spread_bf = spread.astype(BF16)
     tri = (iota((TOK, TOK), 0) >= iota((TOK, TOK), 1)) & ((iota((TOK, TOK), 0) >> 6) == (iota((TOK, TOK), 1) >> 6))
     tri = tri.astype(F32).astype(BF16)
     lane = iota((TOK, 128), 1)
 
     def decay_sums(s):
         rows = pl.ds(s * TOK, TOK)
-        r_bf = dot_t(u_v[rows, :], wt_v[2 * NST:, :]).astype(BF16)
-        pre = dot(r_bf, spread_bf) + bias3
+        pre = dot_t(u_v[rows, :], wr_v[...]).astype(BF16).astype(F32) + bias3
         dt = jnp.maximum(pre, 0.0) + jnp.log1p(jnp.exp(-jnp.abs(pre)))
         part = dot(tri, split3(dt * aneg3, lane))
         cum = (part + pltpu.roll(part, 96, 1)) + pltpu.roll(part, 64, 1)
@@ -132,7 +137,7 @@
 
     def block_scores(s):
         rows = pl.ds(s * TOK, TOK)
-        bc = dot_t(u_v[rows, :], wt_v[:2 * NST, :])
+        bc = dot_t(u_v[rows, :], wt_v[...])
         b_v[rows, :] = bc[:, :NST].astype(BF16)
         c_v[rows, :] = bc[:, NST:].astype(BF16)
         for b in range(NBLK):
@@ -143,17 +148,18 @@
             bt_v[i] = bb.astype(F32).T.astype(BF16)
 
     decay_sums(0)
-    decay_sums(1)
     block_scores(0)
 
-    def proj_x(ch):
+    def proj_x(ch, start=0, count=ROWS):
         cols = pl.ds(ch * CHW, CHW)
-        xs_v[:, cols] = dot_t(u_v[...], wx_v[cols, :]).astype(BF16)
-
-    def head_spread(ch):
+        rows = pl.ds(start, count)
+        xs_v[rows, cols] = dot_t(u_v[rows, :], wx_v[cols, :]).astype(BF16)
+
+    def head_spread(s, ch):
         cols = pl.ds(ch * CHW, CHW)
-        ec_v[:, cols] = dot(csp_v[...], e4_v[:, cols])
-        de_v[:, cols] = dot(dsp_v[...], e4_v[:, cols])
+        rows = pl.ds(s * TOK, TOK)
+        ec_v[rows, cols] = dot(csp_v[rows, :], e4_v[:, cols])
+        de_v[2 * s + ch % 2] = dot(dsp_v[rows, :], e4_v[:, cols])
 
     t_idx = iota((BLK, GW), 0)
     s_idx = iota((BLK, GW), 1) & (BLK - 1)
@@ -166,7 +172,7 @@
                 off = half * GW
                 cols = pl.ds(ch * CHW + off, GW)
                 ce = ec_v[rows, cols]
-                de = de_v[rows, cols]
+                de = de_v[2 * s + ch % 2, b * BLK:(b + 1) * BLK, :]
                 crow = jnp.sum(jnp.where(t_idx == s_idx, ce, 0.0), axis=0, keepdims=True)
                 drow = jnp.sum(jnp.where(t_idx == s_idx, de, 0.0), axis=0, keepdims=True)
                 decay = jnp.exp(jnp.where(t_idx >= s_idx, ce - crow, -jnp.inf))
@@ -215,9 +221,10 @@
         cols = pl.ds(ch * CHW, CHW)
         z_v[:, cols] = dot_t(u_v[...], wz_v[cols, :]).astype(BF16)
 
-    proj_x(0)
-    head_spread(0)
+    proj_x(0, 0, TOK)
+    head_spread(0, 0)
     ssd_blocks(0, 0)
+
     @pl.when(me == 0)
     def _():
         pl.semaphore_wait(barrier, 3)
@@ -227,19 +234,29 @@
     def _():
         pl.semaphore_wait(barrier, 3)
 
+    copies['xb'].wait()
+    norm_rows(TOK, TOK)
     copies['wx1'].wait()
     load('wout', wout_h, wout_v, 6)
     load('up', up1_h, up_v, 7)
     proj_x(1)
-    head_spread(1)
-    block_scores(1)
+    head_spread(0, 1)
+    decay_sums(1)
     for ch in range(1, NCH):
         if ch + 1 < NCH:
-            proj_x(ch + 1)
-            head_spread(ch + 1)
+            if ch >= 2:
+                proj_x(ch + 1)
+            else:
+                proj_x(0, TOK, TOK)
+            head_spread(0, ch + 1)
+        else:
+            block_scores(1)
+            head_spread(1, 0)
         ssd_blocks(0, ch)
         first_send(0, ch)
         relay(0, ch - 1)
+        if ch == 1:
+            proj_x(2)
     load('down', down1_h, down_v, 8)
     load('wq', wq_h, wqkv_v.at[pl.ds(0, QH * HD), :], 9)
     load('wkv', wkv_h, wqkv_v.at[pl.ds(QH * HD, 256), :], 10)
@@ -250,6 +267,8 @@
     copies['wz'].wait()
     for ch in range(NCH):
         proj_z(ch)
+        if ch + 1 < NCH:
+            head_spread(1, ch + 1)
         ssd_blocks(1, ch)
         first_send(1, ch)
         if ch == 0:
@@ -379,13 +398,13 @@
         causal = iota((TOK, TOK), 0) <= iota((TOK, TOK), 1)
 
         def score(h):
-            sc_v[h] = dot(kv_v[s, piece], qz_v[h])
+            sc_v[h % 4] = dot(kv_v[s, piece], qz_v[h])
 
         def soft(h):
             pieces = range(TOK // 64)
 
             def load_scores(r):
-                sc = sc_v[h, r * 64:(r + 1) * 64, :]
+                sc = sc_v[h % 4, r * 64:(r + 1) * 64, :]
                 return jnp.where(causal[r * 64:(r + 1) * 64], sc, -jnp.inf) if first else sc
 
             top = jnp.concatenate([jnp.max(load_scores(r).reshape(8, 8, TOK), axis=0) for r in pieces], axis=0)
@@ -399,7 +418,7 @@
             for r in pieces:
                 prob = jnp.exp(load_scores(r) - top)
                 total = total + jnp.sum(prob.reshape(8, 8, TOK), axis=0)
-                pr_v[h, r * 64:(r + 1) * 64, :] = prob.astype(BF16)
+                pr_v[h % 4, r * 64:(r + 1) * 64, :] = prob.astype(BF16)
             total = jnp.sum(total, axis=0, keepdims=True)
             l_v[h] = total if first else l_v[h] * fix + total
             m_v[h] = top
@@ -407,7 +426,7 @@
 
         def mix(h, fix):
             g = h // 4
-            out = dot(vt_v[s, piece, g * HD:(g + 1) * HD, :], pr_v[h])
+            out = dot(vt_v[s, piece, g * HD:(g + 1) * HD, :], pr_v[h % 4])
             acc_v[h] = out if first else acc_v[h] * fix + out
 
         score(0)
@@ -504,17 +523,17 @@
         in_specs=[any_spec, any_spec, vm_spec, vm_spec, vm_spec] + [any_spec] * 10,
         out_specs=any_spec,
         scratch_shapes=[
-            vm((ROWS, D), BF16), vm((ROWS, D), BF16), vm((INNER, D), BF16), vm((INNER, D), BF16), vm((2 * NST + HEADS, D), BF16),
+            vm((ROWS, D), BF16), vm((ROWS, D), BF16), vm((INNER, D), BF16), vm((INNER, D), BF16), vm((2 * NST, D), BF16), vm((128, D), BF16),
             vm((INNER, D), BF16), vm((D, 2 * FF), BF16), vm((FF, D), BF16), vm((QH * HD + 256, D), BF16), vm((QH * HD, D), BF16),
             vm((32, TOK), F32), vm((32, TOK), F32),
             vm((ROWS, INNER), BF16), vm((ROWS, INNER), BF16), vm((ROWS, NST), BF16), vm((ROWS, NST), BF16),
             vm((ROWS, 128), BF16), vm((ROWS, 128), BF16), vm((128, INNER), BF16), vm((GW, GW), BF16),
-            vm((ROWS, INNER), F32), vm((ROWS, INNER), F32), vm((ROWS, INNER), F32), vm((NSEQ * NBLK * 8, INNER), F32), vm((8, INNER), F32),
+            vm((ROWS, INNER), F32), vm((ROWS, INNER), F32), vm((2 * NSEQ, TOK, CHW), F32), vm((NSEQ * NBLK * 8, INNER), F32), vm((8, INNER), F32),
             vm((NSEQ * NBLK, NCH, NST, CHW), F32), vm((NSEQ, NCH, NST, CHW), F32), vm((NSEQ, NCH, NST, CHW), F32), vm((ROWS, FF), BF16),
             vm((QH, 2 * HD, TOK), BF16), vm((NSEQ, 4, TOK, 128), BF16), vm((NSEQ, 4, 128, TOK), BF16),
             vm((QH, 1, TOK), F32), vm((QH, 1, TOK), F32), vm((QH, HD, TOK), F32), vm((TOK, QH * HD), BF16),
-            vm((QH, TOK, TOK), F32), vm((QH, TOK, TOK), BF16), vm((ROWS, GW), F32), vm((NSEQ * NBLK, NST, BLK), BF16),
-            pltpu.SemaphoreType.DMA((14,)), pltpu.SemaphoreType.DMA((4,)), pltpu.SemaphoreType.DMA((NSEQ, NCH)), pltpu.SemaphoreType.DMA((NSEQ, NCH)),
+            vm((4, TOK, TOK), F32), vm((4, TOK, TOK), BF16), vm((ROWS, GW), F32), vm((NSEQ * NBLK, NST, BLK), BF16),
+            pltpu.SemaphoreType.DMA((17,)), pltpu.SemaphoreType.DMA((4,)), pltpu.SemaphoreType.DMA((NSEQ, NCH)), pltpu.SemaphoreType.DMA((NSEQ, NCH)),
             pltpu.SemaphoreType.DMA((NSEQ, 2)), pltpu.SemaphoreType.DMA((NSEQ, 4)), pltpu.SemaphoreType.DMA((NSEQ, 2)), pltpu.SemaphoreType.DMA((NSEQ, 4)),
         ],
         compiler_params=pltpu.CompilerParams(collective_id=0, has_side_effects=True, vmem_limit_bytes=67_000_000),

time: 54 us -> 52.6 us (0.974)
  Pallas kernels: 51.6 us -> 50.2 us
    pallas_call x1, Pallas kernels: 51.6 us -> 50.2 us  [local_fn(): call(x_loc.reshape(ROWS, D), w_in.T, dt_bias.reshape(1, HEADS), a_neg.res...]
where the time goes in v4:
time: 52.6 us; the launch traced here: 52.4 us
  Pallas kernels  50.2 us (95%)
  local copies, waits for them, and re-layouts  2.26 us (4%)
    pallas_call x1, Pallas kernels, local_fn(): call(x_loc.reshape(ROWS, D), w_in.T, dt_bias.reshape(1, HEADS), a_neg.res...  50.2 us
    unnamed x1, local copies, waits for them, and re-layouts  2.26 us

profile of v4, /device:TPU:7, one launch (start us, length us, event | category | flops | bytes accessed | tf_op | source)
XLA Modules:
  0.0 52.4 jit_solution(10713177955019498622)
XLA Ops:
  0.0 50.2 %layer_stack.1 = bf16[512,1024]{1,0:T(8,128)(2,1)} custom-call(bf16[512,1024]{1,0:T(8,128)(2,1)} %bitcast.15, bf16[3352,1024]{1,0:T(8,128)(2,1)} %bitcast.13, f32[1,24]{1,0:T(1,128)} %bitcast.19, f32[1,24]{1,0:T(1,128)} %bitcast.20, f32[1,24]{1,0:T(1,128)} %bitcast.21, bf16[1536,1024]{1,0:T(8,128)(2,1)} %wout_h.1, bf16[1024,4096]{1,0:T(8,128)(2,1)} %up1_h.1, ...), custom_call_target="tpu_custom_call" | custom-call | tf_op jit(solution)/shard_map/layer_stack/pallas_call | solution.py:546
  50.2 2.3 %copy.17 = bf16[2,256,1024]{2,1,0:T(8,128)(2,1)} copy(bf16[2,256,1024]{2,1,0:T(8,128)(2,1)} %bitcast.14) | data formatting | bytes 2097152
